TPU v7x, 256 devices: a whole 4x4x8 slice. The times are simulated.
256 devices in a mesh: store: 4 (over x), row: 4 (over y_lo, core), col: 16 (over z, y_hi).
Axes of the slice: x: 4, y: 4 (y_hi: 2, y_lo: 2; y = y_hi * 2 + y_lo), z: 8, core: 2. Of those that a mesh axis runs over, the one named last changes fastest.
Arguments:
- tokens: bfloat16 [4096, 6144], P(('store', 'col'), 'row'), may hold values from -24 to 24
- ln_gain: bfloat16 [6144], P('row'), may hold values from 0.099609375 to 1.8984375
- qkv_weight: bfloat16 [6144, 3, 32, 128], P('row', None, 'col', 'store'), may hold values from -0.076546554 to 0.076546554
- q_gain: bfloat16 [128], replicated, may hold values from 0.5 to 7
- k_gain: bfloat16 [128], replicated, may hold values from 0.5 to 7
- out_weight: bfloat16 [32, 128, 6144], P('col', 'store', 'row'), may hold values from -0.09375 to 0.09375
- mlp_in: bfloat16 [6144, 12288], P('row', ('store', 'col')), may hold values from -0.078125 to 0.078125
- mlp_bias: bfloat16 [12288], P(('store', 'col')), may hold values from -3 to 3
- mlp_out: bfloat16 [12288, 6144], P(('store', 'col'), 'row'), may hold values from -0.0546875 to 0.0546875
- out_bias: bfloat16 [6144], P('row'), may hold values from -3 to 3
Outputs:
- mixed: float32 [4096, 6144], P(('store', 'col'), 'row')
All inputs are finite; a program needn't handle non-finite values.
Results may differ from a plain program's by a relative error of at most 0.0059.
Values may be sent and summed in bfloat16 or wider, within the bound.
A program may use at most 64 MiB of HBM per device.

v0:
```python
import math

import jax
import jax.numpy as jnp
from jax import lax
from jax.sharding import Mesh
from jax.sharding import PartitionSpec as P

D = 6144
HD = 128
PATCHES = 256
COL = ("col_0", "col_1")
STORE_COL = ("store", "col_0", "col_1")


epsilon = 1e-06


def copy_for_each(value, axis):
    copies = jnp.broadcast_to(value, (lax.axis_size(axis), *value.shape))
    return lax.all_to_all(copies, axis, split_axis=0, concat_axis=0, tiled=True)


def over_copies(value, axis):
    return copy_for_each(value, axis).sum(axis=0)


def packed_total(arrays, axis):
    ends = [0]
    for a in arrays:
        ends.append(ends[-1] + a.size)
    total = over_copies(jnp.concatenate([a.ravel() for a in arrays]), axis)
    return tuple((total[b:e].reshape(a.shape) for a, b, e in zip(arrays, ends, ends[1:])))


def laid_out(tiles, dim):
    tiles = jnp.moveaxis(tiles, 0, dim)
    shape = tiles.shape
    return tiles.reshape(*shape[:dim], shape[dim] * shape[dim + 1], *shape[dim + 2 :])


def gather_directly(value, axis, dim):
    return laid_out(copy_for_each(value, axis), dim)


def sent_together(arrays, axis, dim, along):
    widths = [math.prod(a.shape[along:]) for a in arrays]
    both = jnp.concatenate(
        [a.reshape(*a.shape[:along], w) for a, w in zip(arrays, widths)], axis=along
    )
    result = lax.all_gather(both, axis, axis=dim, tiled=True)
    tiles = jnp.split(result, [sum(widths[:k]) for k in range(1, len(widths))], axis=along)
    return tuple(
        (b.reshape(*result.shape[:along], *a.shape[along:]) for a, b in zip(arrays, tiles))
    )


def in_one_piece(arrays, axis, dim, along):
    both = jnp.concatenate(arrays, axis=along)
    result, at, finished = (lax.psum_scatter(both, axis, scatter_dimension=dim, tiled=True), 0, [])
    for a in arrays:
        finished.append(lax.slice_in_dim(result, at, at + a.shape[along], axis=along))
        at += a.shape[along]
    return tuple(finished)


def in_one_piece_2(arrays, axis, dim, along):
    ends, at = ([], 0)
    for a in arrays[:-1]:
        at += a.shape[along]
        ends.append(at)
    both = jnp.concatenate(arrays, axis=along)
    return tuple(jnp.split(lax.all_gather(both, axis, axis=dim, tiled=True), ends, axis=along))


def own_rows(terms, axes):
    total = terms.astype(jnp.bfloat16)
    for axis in axes:
        total = lax.psum_scatter(total, axis, scatter_dimension=0, tiled=True)
    return total.astype(jnp.float32)


def head_norm(values, gain):
    average = jnp.mean(values, -1, keepdims=True)
    centred = values - average
    spread = jnp.mean(centred * centred, -1, keepdims=True)
    return (centred * lax.rsqrt(spread + epsilon) * gain.astype(jnp.float32)).astype(jnp.bfloat16)


def attend(qkv_rows, q_gain, k_gain):
    images = qkv_rows.shape[0] // PATCHES
    heads_here = qkv_rows.shape[1] // (3 * HD)
    shaped = qkv_rows.reshape(images, PATCHES, 3, heads_here, HD)
    queries = head_norm(shaped[:, :, 0], q_gain)
    key_rows = head_norm(shaped[:, :, 1], k_gain)
    value_rows = shaped[:, :, 2].astype(jnp.bfloat16)
    scores = jnp.einsum(
        "nqhe,nkhe->nhqk", queries, key_rows, preferred_element_type=jnp.float32
    ) * HD ** (-0.5)
    highest = jnp.max(scores, -1, keepdims=True)
    exponent = jnp.exp(scores - highest)
    softmax_w = (exponent / jnp.sum(exponent, -1, keepdims=True)).astype(jnp.bfloat16)
    mixed_heads = jnp.einsum(
        "nhqk,nkhe->nqhe", softmax_w, value_rows, preferred_element_type=jnp.float32
    )
    return mixed_heads.astype(jnp.bfloat16).reshape(images * PATCHES, heads_here * HD)


def per_device(
    tokens, ln_gain, qkv_weight, q_gain, k_gain, out_weight, mlp_in, mlp_bias, mlp_out, out_bias
):
    tok_f32 = tokens.astype(jnp.float32)
    row_sums, row_squares = packed_total(
        (jnp.sum(tok_f32, 1), jnp.sum(tok_f32 * tok_f32, 1)), "row"
    )
    average = row_sums / D
    variance = row_squares / D - average * average
    scaled = (tok_f32 - average[:, None]) * lax.rsqrt(variance + epsilon)[:, None]
    normed = (scaled * ln_gain.astype(jnp.float32)).astype(jnp.bfloat16)
    normed_all = lax.all_gather(normed, COL, axis=0, tiled=True)
    group_rows = normed_all.shape[0]
    pieces = gather_directly(qkv_weight, "store", 3)
    flat = pieces.reshape(pieces.shape[0], -1)
    product = jnp.dot(normed_all, flat, preferred_element_type=jnp.float32)
    qkv_joined = product.reshape(group_rows, pieces.shape[1], pieces.shape[2], pieces.shape[3])
    qkv_part = qkv_joined.reshape(group_rows, -1)
    mlp_part = jnp.dot(
        normed_all, gather_directly(mlp_in, "store", 1), preferred_element_type=jnp.float32
    )
    out_full, w_out_full, bias_full = (
        lax.all_gather(out_weight, "store", axis=1, tiled=True),
        *sent_together((mlp_out, mlp_bias), "store", 0, 1),
    )
    qkv_rows, mlp_rows = in_one_piece((qkv_part, mlp_part), "row", 0, 1)
    attended = attend(qkv_rows, q_gain, k_gain)
    hidden = jax.nn.gelu(mlp_rows + bias_full.astype(jnp.float32), approximate=False).astype(
        jnp.bfloat16
    )
    attn_all, hidden_all = in_one_piece_2((attended, hidden), "row", 0, 1)
    out_flat = out_full.reshape(-1, out_full.shape[2])
    attn_term = jnp.dot(attn_all, out_flat, preferred_element_type=jnp.float32)
    summed = own_rows(
        attn_term + jnp.dot(hidden_all, w_out_full, preferred_element_type=jnp.float32), COL
    )
    return tok_f32 + summed + out_bias.astype(jnp.float32)


def solution(mesh):
    split = Mesh(
        mesh.devices.reshape(mesh.shape["store"], mesh.shape["row"], 8, 2),
        ("store", "row", "col_0", "col_1"),
    )
    placed = (
        P(STORE_COL, "row"),
        P("row"),
        P("row", None, COL, "store"),
        P(),
        P(),
        P(COL, "store", "row"),
        P("row", STORE_COL),
        P(STORE_COL),
        P(STORE_COL, "row"),
        P("row"),
    )
    return jax.shard_map(
        per_device, mesh=split, in_specs=placed, out_specs=P(STORE_COL, "row"), check_vma=False
    )
```

profile of v0, /device:TPU:2, one launch (start us, length us, event | category | flops | bytes accessed | tf_op | source)
XLA Modules:
  0.0 340.5 jit_solution(624880487631601833)
XLA Ops:
  6.5 1.1 convert_reduce_fusion
  7.6 0.1 pad_maximum_fusion.3
  7.7 0.6 broadcast_in_dim.6
  8.3 3.2 all-to-all-start
  11.5 0.0 all-gather.4.cloned.1.call-start
  11.6 0.7 convert_element_type.70
  12.3 2.9 all-to-all-done
  15.2 0.1 slice_multiply_fusion
  15.3 1.7 fusion.20
  17.0 0.0 all-gather.4.cloned.1.call-update
  17.1 2.8 broadcast_in_dim.7
  19.8 6.0 %all-to-all-start.1 = ((bf16[4,1536,3,2,32]{1,4,3,2,0:T(8,128)(2,1)}), bf16[4,1536,3,2,32]{1,4,3,2,0:T(8,128)(2,1)S(1)}, u32[]{:S(2)}, u32[]{:S(2)}) async-start(bf16[4,1536,3,2,32]{1,4,3,2,0:T(8,128)(2,1)} %broadcast_in_dim.7), calls=%async_computation.1 | async-start | bytes 4718592 | tf_op jit(solution)/shard_map/all_to_all | solution.py:21
  25.8 0.1 reshape.157
  25.9 0.9 pad_maximum_fusion.1
  26.8 0.0 all-gather.6.cloned.1.call-update
  26.8 26.9 %all-to-all-done.1 = bf16[4,1536,3,2,32]{1,4,3,2,0:T(8,128)(2,1)S(1)} async-done(((bf16[4,1536,3,2,32]{1,4,3,2,0:T(8,128)(2,1)}), bf16[4,1536,3,2,32]{1,4,3,2,0:T(8,128)(2,1)S(1)}, u32[]{:S(2)}, u32[]{:S(2)}) %all-to-all-start.1) | async-done | bytes 2359328 | tf_op jit(solution)/shard_map/all_to_all | solution.py:21
  53.7 1.7 broadcast_in_dim.8
  55.4 5.9 %all-to-all-start.2 = ((bf16[4,1536,192]{1,2,0:T(8,128)(2,1)}), bf16[4,1536,192]{1,2,0:T(8,128)(2,1)}, u32[]{:S(2)}, u32[]{:S(2)}) async-start(bf16[4,1536,192]{1,2,0:T(8,128)(2,1)} %broadcast_in_dim.8), calls=%async_computation.2 | async-start | bytes 4718592 | tf_op jit(solution)/shard_map/all_to_all | solution.py:21
  61.3 1.7 copy.31
  63.0 49.6 %all-gather.4.cloned.1.call-done = bf16[1024,1536]{1,0:T(8,128)(2,1)} async-done(((bf16[64,1536]{1,0:T(8,128)(2,1)}), bf16[1024,1536]{1,0:T(8,128)(2,1)}) %all-gather.4.cloned.1.call-update) | async-done | bytes 3145744 | tf_op jit(solution)/shard_map/all_gather | solution.py:120
  112.6 5.2 %fusion.45 = f32[1024,768]{0,1:T(8,128)S(1)} fusion(bf16[1024,1536]{1,0:T(8,128)(2,1)} %all-gather.4.cloned.1.call-done, bf16[1536,768]{0,1:T(8,128)(2,1)} %bitcast.59), kind=kOutput, calls=%fused_computation.78 | convolution fusion | flops 2415919104 | bytes 8650752 | tf_op jit(solution)/shard_map/dot_general | solution.py:124
  117.8 5.2 %fusion.46 = f32[1024,768]{0,1:T(8,128)S(1)} fusion(bf16[1024,1536]{1,0:T(8,128)(2,1)} %all-gather.4.cloned.1.call-done, bf16[1536,768]{0,1:T(8,128)(2,1)} %bitcast.4), kind=kOutput, calls=%fused_computation.79 | convolution fusion | flops 2415919104 | bytes 8650752 | tf_op jit(solution)/shard_map/dot_general | solution.py:127
  123.1 3.3 pad_maximum_fusion
  126.3 0.0 reduce-scatter.4.cloned.1.call-update
  126.4 0.0 all-gather.8.cloned.1.call-start
  126.4 0.6 copy-done.6
  127.0 0.0 copy-done.7
  127.0 20.3 %all-gather.6.cloned.1.call-done = bf16[768,1537]{1,0:T(8,128)(2,1)} async-done(((bf16[192,1537]{1,0:T(8,128)(2,1)}), bf16[768,1537]{1,0:T(8,128)(2,1)}) %all-gather.6.cloned.1.call-update) | async-done | bytes 2360848 | tf_op jit(solution)/shard_map/all_gather | solution.py:51
  147.3 1.1 convert_reduce_fusion.1
  148.4 67.5 %reduce-scatter.4.cloned.1.call-done = f32[256,1536]{0,1:T(8,128)} async-done(((f32[1024,1536]{0,1:T(8,128)}), f32[256,1536]{0,1:T(8,128)}) %reduce-scatter.4.cloned.1.call-update) | async-done | bytes 1572880 | tf_op jit(solution)/shard_map/reduce_scatter | solution.py:60
  215.9 3.3 fusion.43
  219.2 0.1 fusion.28
  219.3 0.3 convolution_multiply_fusion
  219.7 0.2 fusion.44
  219.8 0.3 convolution_convert_fusion
  220.1 0.8 pad_maximum_fusion.2
  220.9 0.0 all-gather.8.cloned.1.call-update
  221.0 0.0 reduce-scatter.6.cloned.1.call-start
  221.0 14.2 %all_gather.15 = bf16[2,128,1536]{2,1,0:T(8,128)(2,1)S(1)} all-gather(bf16[2,32,1536]{2,1,0:T(8,128)(2,1)S(1)} %copy-done.3), channel_id=1, replica_groups=mesh['store'=4,'row'=4,'col_0'=8,'col_1'=2] {'store'}, dimensions={1}, use_global_device_ids=true | all-gather | bytes 983040 | tf_op jit(solution)/shard_map/all_gather | solution.py:131
  235.2 17.1 %all-gather.8.cloned.1.call-done = bf16[1024,1024]{0,1:T(8,128)(2,1)} async-done(((bf16[256,1024]{0,1:T(8,128)(2,1)}), bf16[1024,1024]{0,1:T(8,128)(2,1)}) %all-gather.8.cloned.1.call-update) | async-done | bytes 2097168 | tf_op jit(solution)/shard_map/all_gather | solution.py:73
  252.3 4.8 %fusion.1 = f32[1024,1536]{1,0:T(8,128)S(1)} fusion(bf16[768,1537]{1,0:T(8,128)(2,1)} %all-gather.6.cloned.1.call-done, bf16[1024,1024]{0,1:T(8,128)(2,1)} %all-gather.8.cloned.1.call-done), kind=kOutput, calls=%fused_computation.3 | convolution fusion | flops 2415919104 | bytes 10223616 | tf_op jit(solution)/shard_map/dot_general | solution.py:143
  257.1 3.7 %add_convert_fusion = bf16[1024,1536]{1,0:T(8,128)(2,1)} fusion(f32[1024,1536]{1,0:T(8,128)S(1)} %fusion.1, bf16[256,1536]{1,0:T(8,128)(2,1)S(1)} %bitcast.58, bf16[1024,1024]{0,1:T(8,128)(2,1)} %all-gather.8.cloned.1.call-done), kind=kOutput, calls=%fused_computation.2 | convolution fusion | flops 808452096 | bytes 10747904 | tf_op jit(solution)/shard_map/dot_general | solution.py:141
  260.9 0.0 reduce-scatter.6.cloned.1.call-update
  260.9 0.0 reduce-scatter.8.cloned.1.call-start
  260.9 49.5 %reduce-scatter.6.cloned.1.call-done = bf16[128,1536]{1,0:T(8,128)(2,1)} async-done(((bf16[1024,1536]{1,0:T(8,128)(2,1)}), bf16[128,1536]{1,0:T(8,128)(2,1)}) %reduce-scatter.6.cloned.1.call-update) | async-done | bytes 393232 | tf_op jit(solution)/shard_map/reduce_scatter | solution.py:79
  310.4 0.0 reduce-scatter.8.cloned.1.call-update
  310.4 21.5 %reduce-scatter.8.cloned.1.call-done = bf16[64,1536]{1,0:T(8,128)(2,1)} async-done(((bf16[128,1536]{1,0:T(8,128)(2,1)}), bf16[64,1536]{1,0:T(8,128)(2,1)}) %reduce-scatter.8.cloned.1.call-update) | async-done | bytes 196624 | tf_op jit(solution)/shard_map/reduce_scatter | solution.py:79
  332.0 1.7 fusion.21
  (25 shorter events, 0.1 us)
Async XLA Ops:
  8.3 6.9 %all-to-all-start = ((f32[4,1,128]{2,1,0:T(1,128)}), f32[4,1,128]{2,1,0:T(1,128)S(1)}, u32[]{:S(2)}, u32[]{:S(2)}) async-start(f32[4,1,128]{2,1,0:T(1,128)} %broadcast_in_dim.6), calls=%async_computation | async-start | bytes 4096 | tf_op jit(solution)/shard_map/all_to_all | solution.py:21
  11.5 101.1 %all-gather.4.cloned.1.call-start = ((), (), s32[]{:S(2)}) async-start(), calls=%async_computation.6 | async-start | bytes 3342336 | tf_op jit(solution)/shard_map/all_gather | solution.py:120
  19.8 6.0 %copy-start.5 = (bf16[192]{0:T(256)(128)(2,1)S(1)}, bf16[192]{0:T(256)(128)(2,1)}, u32[]{:S(2)}) copy-start(bf16[192]{0:T(256)(128)(2,1)} %param.17) | copy-start | bytes 1156
  19.8 6.1 %copy-start.1 = (bf16[192,1536]{1,0:T(8,128)(2,1)S(1)}, bf16[192,1536]{1,0:T(8,128)(2,1)}, u32[]{:S(2)}) copy-start(bf16[192,1536]{1,0:T(8,128)(2,1)} %param.18) | copy-start | bytes 1769476
  19.8 33.9 %copy-start.2 = (bf16[1536,192]{0,1:T(8,128)(2,1)S(1)}, bf16[1536,192]{0,1:T(8,128)(2,1)}, u32[]{:S(2)}) copy-start(bf16[1536,192]{0,1:T(8,128)(2,1)} %param.16) | copy-start | bytes 1769476
  19.8 33.9 %all-to-all-start.1 = ((bf16[4,1536,3,2,32]{1,4,3,2,0:T(8,128)(2,1)}), bf16[4,1536,3,2,32]{1,4,3,2,0:T(8,128)(2,1)S(1)}, u32[]{:S(2)}, u32[]{:S(2)}) async-start(bf16[4,1536,3,2,32]{1,4,3,2,0:T(8,128)(2,1)} %broadcast_in_dim.7), calls=%async_computation.1 | async-start | bytes 4718592 | tf_op jit(solution)/shard_map/all_to_all | solution.py:21
  25.8 121.5 %all-gather.6.cloned.1.call-start = ((), (), s32[]{:S(2)}) async-start(), calls=%async_computation.8 | async-start | bytes 3194880 | tf_op jit(solution)/shard_map/all_gather | solution.py:51
  55.4 62.4 %all-to-all-start.2 = ((bf16[4,1536,192]{1,2,0:T(8,128)(2,1)}), bf16[4,1536,192]{1,2,0:T(8,128)(2,1)}, u32[]{:S(2)}, u32[]{:S(2)}) async-start(bf16[4,1536,192]{1,2,0:T(8,128)(2,1)} %broadcast_in_dim.8), calls=%async_computation.2 | async-start | bytes 4718592 | tf_op jit(solution)/shard_map/all_to_all | solution.py:21
  61.3 154.5 %reduce-scatter.4.cloned.1.call-start = ((), (), s32[]{:S(2)}) async-start(), calls=%async_computation.7 | async-start | bytes 7864320 | tf_op jit(solution)/shard_map/reduce_scatter | solution.py:60
  126.3 0.7 copy-start.6
  126.3 0.7 copy-start.7
  126.4 126.0 %all-gather.8.cloned.1.call-start = ((), (), s32[]{:S(2)}) async-start(), calls=%async_computation.9 | async-start | bytes 2621440 | tf_op jit(solution)/shard_map/all_gather | solution.py:73
  219.3 1.7 copy-start.3
  221.0 89.4 %reduce-scatter.6.cloned.1.call-start = ((), (), s32[]{:S(2)}) async-start(), calls=%async_computation.10 | async-start | bytes 3538944 | tf_op jit(solution)/shard_map/reduce_scatter | solution.py:79
  260.9 49.6 %copy-start.4 = (bf16[1536]{0:T(1024)(128)(2,1)S(1)}, bf16[1536]{0:T(1024)(128)(2,1)}, u32[]{:S(2)}) copy-start(bf16[1536]{0:T(1024)(128)(2,1)} %param.19) | copy-start | bytes 9220
  260.9 71.1 %copy-start = (bf16[64,1536]{1,0:T(8,128)(2,1)S(1)}, bf16[64,1536]{1,0:T(8,128)(2,1)}, u32[]{:S(2)}) copy-start(bf16[64,1536]{1,0:T(8,128)(2,1)} %param.10) | copy-start | bytes 589828
  260.9 71.1 %reduce-scatter.8.cloned.1.call-start = ((), (), s32[]{:S(2)}) async-start(), calls=%async_computation.11 | async-start | bytes 589824 | tf_op jit(solution)/shard_map/reduce_scatter | solution.py:79
Sparse Core Ops, SparseCore 0:
  17.2 95.3 all-gather.3
  114.4 32.8 all-gather.5
  149.9 65.9 reduce-scatter.3
  221.1 31.2 all-gather.7
  261.0 49.3 reduce-scatter.5
  312.7 19.1 reduce-scatter.7
where the time goes:
time: 342 us; the launch traced here: 341 us
  waiting for transfers between devices  255 us (75%)
  matrix products  19.6 us (6%)
  starting transfers between devices  15.3 us (4%)
  other arithmetic  15 us (4%)
  blocking collectives  14.2 us (4%)
  between operations  13.6 us (4%)
  local copies, waits for them, and re-layouts  7.4 us (2%)
    reduce_scatter x2, waiting for transfers between devices, own_rows(): total = lax.psum_scatter(total, axis, scatter_dimension=0, tiled=True)  71 us
    reduce_scatter x1, waiting for transfers between devices, in_one_piece(): lax.psum_scatter(both, axis, scatter_dimension=dim, tiled=True)  67.5 us
    all_gather x1, waiting for transfers between devices, per_device(): normed_all = lax.all_gather(normed, COL, axis=0, tiled=True)  49.6 us
    all_to_all x3, waiting for transfers between devices, copy_for_each(): return lax.all_to_all(copies, axis, split_axis=0, concat_axis=0, tiled=True)  29.9 us
    all_gather x1, waiting for transfers between devices, sent_together(): result = lax.all_gather(both, axis, axis=dim, tiled=True)  20.3 us
    all_gather x1, waiting for transfers between devices, in_one_piece_2(): lax.all_gather(both, axis, axis=dim, tiled=True)  17.1 us
    all_to_all x3, starting transfers between devices, copy_for_each(): return lax.all_to_all(copies, axis, split_axis=0, concat_axis=0, tiled=True)  15.1 us
    all_gather x1, blocking collectives, per_device(): lax.all_gather(out_weight, 'store', axis=1, tiled=True)  14.2 us
  transfers between devices with their start and end apart: 9, of which 8 were waited for; matrix products, arithmetic and copies ran while one was open for 7% of the time, Pallas kernels for 0%

commit v1 on v0

v1 whole, which is shorter than its diff:
```python
import functools

import jax
import jax.numpy as jnp
from jax import lax
from jax.experimental import pallas as pl
from jax.experimental.pallas import tpu as pltpu
from jax.sharding import Mesh
from jax.sharding import PartitionSpec as P

D = 6144
HD = 128
IMAGE = 256
NX, NZ = 4, 8
BLOCK = 64
ROWS = 1024
PIECE = 1536
HALF = 768
UNITS = 96
EPS = 1e-06
MESH = pl.DeviceIdType.MESH
F32, BF16 = jnp.float32, jnp.bfloat16
NT = (((1,), (1,)), ((), ()))


class Names:
    def __init__(self):
        self.index = {}

    def __call__(self, *key):
        return self.index.setdefault(key, len(self.index))


N_SEMS = 224
N_LOCAL = 8


def kernel(
    tok, ln_gain, wq, wm, q_gain, k_gain, ow, bias, mo, out_bias,
    out,
    stats, stats_in, xg, WQ, WM, BI, OW, MO, hp, hx, att, part,
    zs, zr, ns, nr, ws, wr, send, recv, local,
):
    x, yl, k = lax.axis_index("x"), lax.axis_index("yl"), lax.axis_index("k")
    z, yh = lax.axis_index("z"), lax.axis_index("yh")
    nl, nk, nh = 1 - yl, 1 - k, 1 - yh
    xs = [lax.rem(x + d, NX) for d in range(NX)]
    zn = [lax.rem(z + d, NZ) for d in range(NZ)]
    at_x = lambda d: {"x": xs[d % NX]}
    at_z = lambda d: {"z": zn[d % NZ]}
    flip_l = {"yl": nl}
    flip_lh = {"yl": nl, "yh": nh}
    partner = {"k": nk}
    flip_lk = {"yl": nl, "k": nk}
    rel_l, rel_h = (yl, nl, nl, yl), (yh, yh, nh, nh)

    name, started = Names(), []

    def push(key, src, dst, peer):
        i = name(*key)
        copy = pltpu.make_async_remote_copy(
            src_ref=src, dst_ref=dst, send_sem=send.at[i], recv_sem=recv.at[i],
            device_id=peer, device_id_type=MESH,
        )
        copy.start()
        started.append(copy)

    def take(key, dst):
        i = name(*key)
        pltpu.make_async_remote_copy(
            src_ref=dst, dst_ref=dst, send_sem=send.at[i], recv_sem=recv.at[i],
            device_id=partner, device_id_type=MESH,
        ).wait_recv()

    barrier = pltpu.get_barrier_semaphore()
    peers = [at_x(1), at_x(-1), at_x(2), at_z(1), at_z(-1), flip_l, flip_lh, partner, flip_lk]
    for peer in peers:
        pl.semaphore_signal(barrier, inc=1, device_id=peer, device_id_type=MESH)

    t = tok[...].astype(F32)
    s1 = jnp.sum(t, 1, keepdims=True)
    s2 = jnp.sum(t * t, 1, keepdims=True)
    lane = lax.broadcasted_iota(jnp.int32, (BLOCK, 128), 1)
    stats[...] = jnp.where(lane < 64, s1, s2)
    pl.semaphore_wait(barrier, len(peers))

    def stored(w, j, c):
        if w == 0:
            return wq.at[:, j, :, c]
        return (None, wm, ow, mo)[w].at[j, :, c]

    def gathered(w, q, s, c):
        if w == 0:
            return WQ.at[q, :, s, :, c]
        return (None, WM, OW, MO)[w].at[q, s, :, c]

    full, halves = pl.ds(0, PIECE), (pl.ds(0, HALF), pl.ds(HALF, HALF))
    local_copies = []

    def x_push(w, q):
        qq = (yl, nl)[q]
        dst = gathered(w, qq, x, full)
        for d in (1, -1):
            push(("x", w, q, d), stored(w, yl, full) if q == 0 else dst, dst, at_x(d))

    def x_relay(w, q):
        qq = (yl, nl)[q]
        for d in (1, -1):
            take(("x", w, q, d), gathered(w, qq, xs[-d % NX], full))
            c = halves[0 if d == 1 else 1]
            ref = gathered(w, qq, xs[-d % NX], c)
            push(("x2", w, q, d), ref, ref, at_x(d))

    def x_last(w, q):
        qq = (yl, nl)[q]
        for d in (1, -1):
            c = halves[0 if d == 1 else 1]
            take(("x2", w, q, d), gathered(w, qq, xs[2], c))

    def w_send(w, h):
        push(("w", w, h), stored(w, nl, halves[h]), gathered(w, yl, x, halves[h]), flip_l)

    def w_take(w):
        for h in range(2):
            take(("w", w, h), gathered(w, nl, x, halves[h]))

    for i, peer in enumerate((partner, flip_l, flip_lk)):
        push(("stats", i), stats, stats_in.at[i], peer)
    x_push(0, 0)
    x_push(1, 0)
    w_send(0, 0)
    for d in (1, -1, 2):
        push(("bias", d), bias.at[yl], BI.at[x], at_x(d))
    for w in range(4):
        copy = pltpu.make_async_copy(stored(w, yl, full), gathered(w, yl, x, full), local.at[w])
        copy.start()
        local_copies.append(copy)
    BI[x] = bias[yl]

    for i in range(3):
        take(("stats", i), stats_in.at[i])
    total = stats[...] + stats_in[0] + stats_in[1] + stats_in[2]
    mean = total[:, 0:1] * (1.0 / D)
    var = total[:, 64:65] * (1.0 / D) - mean * mean
    normed = ((t - mean) * lax.rsqrt(var + EPS) * ln_gain[...].astype(F32)).astype(BF16)

    def tokens_at(h, r, zz):
        row = pl.multiple_of((zz * 2 + rel_h[r]) * BLOCK, BLOCK)
        return xg.at[h, rel_l[r], pl.ds(row, BLOCK)]

    def z_half(ref, d):
        return ref.at[pl.ds(0 if d == 1 else BLOCK // 2, BLOCK // 2)]

    own_row = pl.multiple_of((z * 2 + yh) * BLOCK, BLOCK)
    xg[0, yl, pl.ds(own_row, BLOCK)] = normed[:, :HALF]
    xg[1, yl, pl.ds(own_row, BLOCK)] = normed[:, HALF:]

    def z_push(h, r, d, dist):
        ref = tokens_at(h, r, zn[-d * (dist - 1) % NZ])
        if dist == 4:
            ref = z_half(ref, d)
        push(("z", h, r, d, dist), ref, ref, at_z(d))

    def z_take(h, r, d, dist):
        ref = tokens_at(h, r, zn[-d * dist % NZ])
        if dist == 4:
            ref = z_half(ref, d)
        take(("z", h, r, d, dist), ref)

    def y_push(h, dz):
        ref = tokens_at(h, 0, zn[dz % NZ])
        push(("yl", h, dz % NZ), ref, ref, flip_l)
        push(("yn", h, dz % NZ), ref, ref, flip_lh)

    def y_relay(h, dz):
        ref = tokens_at(h, 1, zn[dz % NZ])
        take(("yl", h, dz % NZ), ref)
        push(("yr", h, dz % NZ), ref, ref, flip_lh)

    def y_last(h, dz):
        take(("yn", h, dz % NZ), tokens_at(h, 2, zn[dz % NZ]))
        take(("yr", h, dz % NZ), tokens_at(h, 3, zn[dz % NZ]))

    def z_step(h, r, dist):
        for d in (1, -1):
            z_take(h, r, d, dist)
            if dist < 4:
                z_push(h, r, d, dist + 1)

    def z_first(h, r):
        for d in (1, -1):
            z_push(h, r, d, 1)

    z_first(0, 0)
    z_first(1, 0)
    y_push(1, 0)
    y_push(0, 0)
    w_send(0, 1)
    w_send(1, 0)

    z_step(0, 0, 1)
    y_relay(1, 0)
    z_first(1, 1)
    take(("yn", 1, 0), tokens_at(1, 2, z))
    z_first(1, 2)
    y_push(0, -1)
    y_push(0, 1)
    w_send(1, 1)
    x_relay(0, 0)
    y_relay(0, 0)
    take(("yr", 1, 0), tokens_at(1, 3, z))
    z_first(1, 3)
    w_take(0)
    x_push(0, 1)
    z_step(1, 0, 1)
    z_step(0, 0, 2)
    y_push(0, -2)
    y_push(0, 2)
    y_relay(0, -1)
    y_relay(0, 1)
    for r in (1, 2, 3):
        z_step(1, r, 1)
    x_relay(1, 0)
    w_take(1)
    x_push(1, 1)
    z_step(0, 0, 3)
    y_push(0, -3)
    y_push(0, 3)
    y_relay(0, -2)
    y_relay(0, 2)
    for r in range(4):
        z_step(1, r, 2)
    z_step(0, 0, 4)
    y_push(0, 4)
    x_relay(0, 1)
    y_relay(0, -3)
    y_relay(0, 3)
    for w in (2, 3):
        for h in range(2):
            w_send(w, h)
    for r in range(4):
        z_step(1, r, 3)
    x_relay(1, 1)
    x_push(2, 0)
    x_push(3, 0)
    y_relay(0, 4)
    for w in (0, 1):
        local_copies[w].wait()
        for q in range(2):
            x_last(w, q)
    for r in range(4):
        z_step(1, r, 4)
    for dz in (0, -1, 1, -2, 2, -3, 3, 4):
        y_last(0, dz)

    def project(i, carry):
        row = pl.multiple_of(lax.rem(i * 256 + nk * 512, ROWS), 256)
        acc_q = jnp.zeros((256, 384), F32)
        acc_m = jnp.zeros((256, 384), F32)
        for q in range(2):
            for h in range(2):
                lhs = xg[h, q, pl.ds(row, 256)]
                cols = slice(h * HALF, (h + 1) * HALF)
                acc_q += lax.dot_general(
                    lhs, WQ[q, :, :, :, cols].reshape(384, HALF), NT, preferred_element_type=F32
                )
                acc_m += lax.dot_general(
                    lhs, WM[q, :, :, cols].reshape(384, HALF), NT, preferred_element_type=F32
                )
        hp[pl.ds(row, 256), pl.ds(0, 384)] = acc_q
        hp[pl.ds(row, 256), pl.ds(384, 384)] = acc_m
        return carry

    lax.fori_loop(0, 2, project, 0)
    theirs = hp.at[pl.ds(pl.multiple_of(nk * 512, 512), 512)]
    push(("hx",), theirs, hx, partner)
    x_relay(2, 0)
    for w in (2, 3):
        w_take(w)
        x_push(w, 1)
    lax.fori_loop(2, 4, project, 0)
    x_relay(3, 0)
    take(("hx",), hx)
    for d in (1, -1, 2):
        take(("bias", d), BI.at[xs[-d % NX]])

    def head_norm(values, gain):
        centred = values - jnp.mean(values, -1, keepdims=True)
        spread = jnp.mean(centred * centred, -1, keepdims=True)
        return (centred * lax.rsqrt(spread + EPS) * gain[...].astype(F32)).astype(BF16)

    def image(i, carry):
        mine = pl.multiple_of(i * IMAGE, IMAGE)
        row = pl.multiple_of(k * 512 + mine, IMAGE)
        joined = hp[pl.ds(row, IMAGE)] + hx[pl.ds(mine, IMAGE)]
        q = head_norm(joined[:, 0:128], q_gain)
        kk = head_norm(joined[:, 128:256], k_gain)
        v = joined[:, 256:384].astype(BF16)
        scores = lax.dot_general(q, kk, NT, preferred_element_type=F32) * HD ** (-0.5)
        e = jnp.exp(scores - jnp.max(scores, -1, keepdims=True))
        probs = (e / jnp.sum(e, -1, keepdims=True)).astype(BF16)
        attended = jnp.dot(probs, v, preferred_element_type=F32)
        att[k, pl.ds(mine, IMAGE), pl.ds(0, 128)] = attended.astype(BF16)
        pre = joined[:, 384:768] + lax.dot_general(
            jnp.ones((IMAGE, 128), BF16), BI[...].reshape(384, 128), NT, preferred_element_type=F32
        )
        hidden = 0.5 * pre * (1.0 + lax.erf(pre * (0.5 ** 0.5)))
        att[k, pl.ds(mine, IMAGE), pl.ds(128, 384)] = hidden.astype(BF16)
        return carry

    lax.fori_loop(0, 2, image, 0)
    push(("att",), att.at[k], att.at[k], partner)
    for w in (2, 3):
        x_relay(w, 1)
    for w in (2, 3):
        local_copies[w].wait()
        for q in range(2):
            x_last(w, q)

    def output_terms(i, carry):
        row = pl.multiple_of(lax.rem(i * 256 + k * 512, ROWS), 256)
        a = att[row // 512, pl.ds(pl.multiple_of(lax.rem(row, 512), 256), 256)]
        for q in range(2):
            for h in range(2):
                cols = slice(h * HALF, (h + 1) * HALF)
                part[q, h, pl.ds(row, 256)] = jnp.dot(
                    a[:, :128], OW[q, :, :, cols].reshape(128, HALF), preferred_element_type=F32
                ) + jnp.dot(
                    a[:, 128:], MO[q, :, :, cols].reshape(384, HALF), preferred_element_type=F32
                )
        return carry

    lax.fori_loop(0, 2, output_terms, 0)
    take(("att",), att.at[nk])
    lax.fori_loop(2, 4, output_terms, 0)

    def term(h, r, dz):
        row = pl.multiple_of((zn[dz % NZ] * 2 + rel_h[r]) * BLOCK, BLOCK)
        return part.at[rel_l[r], h, pl.ds(row, BLOCK)]

    half = BLOCK // 2

    def chain(h, r, d, dist):
        g, di = (0 if h == 0 else 1 + r), (0 if d == 1 else 1)
        blk = term(h, r, d * dist)
        slot, landing = zs.at[g, di, dist - 1], zr.at[g, di, dist - 1]
        lo = 0 if d == 1 else half
        if dist == 4:
            slot, landing = slot.at[pl.ds(0, half)], landing.at[pl.ds(0, half)]
            slot[...] = blk[pl.ds(lo, half)].astype(BF16)
        elif dist == 3:
            before = zr.at[g, di, 3, pl.ds(0, half)]
            take(("c", g, d, 4), before)
            slot[pl.ds(half - lo, half)] = blk[pl.ds(half - lo, half)].astype(BF16)
            slot[pl.ds(lo, half)] = (blk[pl.ds(lo, half)] + before[...].astype(F32)).astype(BF16)
        else:
            before = zr.at[g, di, dist]
            take(("c", g, d, dist + 1), before)
            slot[...] = (blk[...] + before[...].astype(F32)).astype(BF16)
        push(("c", g, d, dist), slot, landing, at_z(d))

    def chains(h, r, dist):
        for d in (1, -1):
            chain(h, r, d, dist)

    def chain_end(h, r):
        g = 0 if h == 0 else 1 + r
        for d in (1, -1):
            take(("c", g, d, 1), zr.at[g, 0 if d == 1 else 1, 0])
        blk = term(h, r, 0)
        blk[...] = blk[...] + zr[g, 0, 0].astype(F32) + zr[g, 1, 0].astype(F32)

    def y_out(h, dz):
        g = dz % NZ if h == 0 else NZ
        for j, r in enumerate((2, 3)):
            ns[g, j] = term(h, r, dz)[...].astype(BF16)
            push(("n", g, j), ns.at[g, j], nr.at[g, j], flip_lh)

    def y_mid(h, dz):
        g = dz % NZ if h == 0 else NZ
        take(("n", g, 1), nr.at[g, 1])
        ws[g] = (term(h, 1, dz)[...] + nr[g, 1].astype(F32)).astype(BF16)
        push(("m", g), ws.at[g], wr.at[g], flip_l)

    def y_end(h, dz):
        g = dz % NZ if h == 0 else NZ
        take(("n", g, 0), nr.at[g, 0])
        take(("m", g), wr.at[g])
        blk = term(h, 0, dz)
        blk[...] = blk[...] + nr[g, 0].astype(F32) + wr[g].astype(F32)

    order = (4, 3, -3, 2, -2, 1, -1, 0)
    for r in range(4):
        chains(1, r, 4)
        y_out(0, order[r])
    for dz in order[4:]:
        y_out(0, dz)
    y_mid(0, 4)
    for r in range(4):
        chains(1, r, 3)
    y_mid(0, 3)
    y_mid(0, -3)
    y_end(0, 4)
    chains(0, 0, 4)
    for r in range(4):
        chains(1, r, 2)
    y_mid(0, 2)
    y_end(0, 3)
    y_end(0, -3)
    chains(0, 0, 3)
    y_mid(0, -2)
    for r in (2, 3, 1, 0):
        chains(1, r, 1)
    y_mid(0, 1)
    y_end(0, 2)
    y_end(0, -2)
    chains(0, 0, 2)
    y_mid(0, -1)
    chain_end(1, 2)
    chain_end(1, 3)
    y_out(1, 0)
    y_mid(0, 0)
    chain_end(1, 1)
    y_mid(1, 0)
    y_end(0, 1)
    y_end(0, -1)
    chains(0, 0, 1)
    chain_end(1, 0)
    y_end(0, 0)
    chain_end(0, 0)
    y_end(1, 0)
    for h in range(2):
        cols = slice(h * HALF, (h + 1) * HALF)
        out[:, cols] = tok[:, cols].astype(F32) + term(h, 0, 0)[...] + out_bias[:, cols].astype(F32)

    for copy in started:
        copy.wait_send()
    assert len(name.index) <= N_SEMS, len(name.index)


def per_device(
    tokens, ln_gain, qkv_weight, q_gain, k_gain, out_weight, mlp_in, mlp_bias, mlp_out, out_bias
):
    wq = jnp.transpose(qkv_weight, (1, 2, 3, 0))
    wm = jnp.transpose(mlp_in).reshape(2, UNITS, PIECE)
    mo = mlp_out.reshape(2, UNITS, PIECE)
    column0 = jnp.arange(128) == 0
    bias = jnp.where(column0, mlp_bias.reshape(2, UNITS, 1), 0).astype(BF16)
    vm, hbm = pl.BlockSpec(memory_space=pltpu.VMEM), pl.BlockSpec(memory_space=pl.ANY)
    block = (BLOCK, HALF)
    return pl.pallas_call(
        kernel,
        out_shape=jax.ShapeDtypeStruct((BLOCK, PIECE), F32),
        in_specs=[vm, vm, hbm, hbm, vm, vm, hbm, vm, hbm, vm],
        out_specs=vm,
        scratch_shapes=[
            pltpu.VMEM((BLOCK, 128), F32),
            pltpu.VMEM((3, BLOCK, 128), F32),
            pltpu.VMEM((2, 2, ROWS, HALF), BF16),
            pltpu.VMEM((2, 3, NX, 32, PIECE), BF16),
            pltpu.VMEM((2, NX, UNITS, PIECE), BF16),
            pltpu.VMEM((NX, UNITS, 128), BF16),
            pltpu.VMEM((2, NX, 32, PIECE), BF16),
            pltpu.VMEM((2, NX, UNITS, PIECE), BF16),
            pltpu.VMEM((ROWS, HALF), F32),
            pltpu.VMEM((512, HALF), F32),
            pltpu.VMEM((2, 512, 512), BF16),
            pltpu.VMEM((2, 2, ROWS, HALF), F32),
            pltpu.VMEM((5, 2, 4, *block), BF16),
            pltpu.VMEM((5, 2, 4, *block), BF16),
            pltpu.VMEM((NZ + 1, 2, *block), BF16),
            pltpu.VMEM((NZ + 1, 2, *block), BF16),
            pltpu.VMEM((NZ + 1, *block), BF16),
            pltpu.VMEM((NZ + 1, *block), BF16),
            pltpu.SemaphoreType.DMA((N_SEMS,)),
            pltpu.SemaphoreType.DMA((N_SEMS,)),
            pltpu.SemaphoreType.DMA((N_LOCAL,)),
        ],
        compiler_params=pltpu.CompilerParams(
            collective_id=0, has_side_effects=True, vmem_limit_bytes=62 * 1024 * 1024
        ),
        name="layer",
    )(
        tokens, ln_gain.reshape(1, PIECE), wq, wm, q_gain.reshape(1, HD), k_gain.reshape(1, HD),
        out_weight, bias, mo, out_bias.reshape(1, PIECE),
    )


def solution(mesh):
    split = Mesh(
        mesh.devices.reshape(NX, 2, 2, NZ, 2), ("x", "yl", "k", "z", "yh")
    )
    token_axes, row, col = ("x", "z", "yh"), ("yl", "k"), ("z", "yh")
    placed = (
        P(token_axes, row),
        P(row),
        P(row, None, col, "x"),
        P(),
        P(),
        P(col, "x", row),
        P(row, token_axes),
        P(token_axes),
        P(token_axes, row),
        P(row),
    )
    return jax.shard_map(
        per_device, mesh=split, in_specs=placed, out_specs=P(token_axes, row), check_vma=False
    )
```

time: 342 us -> 138 us (0.40)
  waiting for transfers between devices: 255 us -> 0 us
  Pallas kernels: 0 us -> 133 us
  matrix products: 19.6 us -> 0 us
  starting transfers between devices: 15.3 us -> 0 us
  other arithmetic: 15 us -> 0.72 us
  blocking collectives: 14.2 us -> 0 us
  between operations: 13.6 us -> 0.02 us
  local copies, waits for them, and re-layouts: 7.4 us -> 3.79 us
    reduce_scatter x3 -> x0, waiting for transfers between devices: 138 us -> none  [the longest x2 71 us: own_rows(): total = lax.psum_scatter(total, axis, scatter_dimension=0, tiled=True)]
    pallas_call x0 -> x1, Pallas kernels: none -> 133 us  [per_device(): pl.pallas_call(kernel, out_shape=jax.ShapeDtypeStruct((BLOCK, PIECE), F32...]
    all_gather x3 -> x0, waiting for transfers between devices: 87 us -> none  [the longest x1 49.6 us: per_device(): normed_all = lax.all_gather(normed, COL, axis=0, tiled=True)]
    all_to_all x3 -> x0, waiting for transfers between devices: 29.9 us -> none  [copy_for_each(): return lax.all_to_all(copies, axis, split_axis=0, concat_axis=0, tiled=True)]
    dot_general x6 -> x0, matrix products: 19.6 us -> none  [the longest x1 5.25 us: per_device(): jnp.dot(normed_all, gather_directly(mlp_in, 'store', 1), preferred_elemen...]
    all_to_all x3 -> x0, starting transfers between devices: 15.1 us -> none  [copy_for_each(): return lax.all_to_all(copies, axis, split_axis=0, concat_axis=0, tiled=True)]
    all_gather x1 -> x0, blocking collectives: 14.2 us -> none  [per_device(): lax.all_gather(out_weight, 'store', axis=1, tiled=True)]
    concatenate x4 -> x0, other arithmetic: 5.06 us -> none  [the longest x1 3.26 us: in_one_piece(): both = jnp.concatenate(arrays, axis=along)]
  transfers between devices with their start and end apart: 9 -> 0, of which waited for: 8 -> 0; matrix products, arithmetic and copies ran while one was open for 7% -> 0% of each run, Pallas kernels for 0% -> 0%
where the time goes in v1:
time: 138 us
  Pallas kernels  133 us (96%)
  local copies, waits for them, and re-layouts  3.79 us (3%)
    pallas_call x1, Pallas kernels, per_device(): pl.pallas_call(kernel, out_shape=jax.ShapeDtypeStruct((BLOCK, PIECE), F32...  133 us

profile of v1, /device:TPU:2, one launch (start us, length us, event | category | flops | bytes accessed | tf_op | source)
XLA Modules:
  0.0 137.7 jit_solution(1094408664459244228)
XLA Ops:
  0.0 0.0 copy-start.2
  0.0 0.0 copy-start
  0.0 0.7 copy-done.2
  0.7 0.1 broadcast_in_dim.19
  0.7 0.0 copy-done
  0.7 0.0 copy-start.1
  0.8 0.6 reshape.20.ln_gain
  1.4 0.1 copy-done.1
  1.4 0.6 reshape.25.out_bias
  2.0 0.7 broadcast_select_fusion.bias
  2.7 133.2 %layer.1 = f32[64,1536]{1,0:T(8,128)} custom-call(bf16[64,1536]{1,0:T(8,128)(2,1)} %tok.1, bf16[1,1536]{1,0:T(2,128)(2,1)} %reshape.20.ln_gain, bf16[3,2,32,1536]{3,2,1,0:T(8,128)(2,1)} %bitcast.7, bf16[2,96,1536]{2,1,0:T(8,128)(2,1)} %bitcast.8, bf16[1,128]{1,0:T(2,128)(2,1)} %bitcast.10, bf16[1,128]{1,0:T(2,128)(2,1)} %bitcast.11, ...), custom_call_target="tpu_custom_call" | custom-call | tf_op jit(solution)/shard_map/layer/pallas_call | solution.py:451
  136.0 1.8 %copy.12 = f32[64,1536]{1,0:T(8,128)} copy(f32[64,1536]{1,0:T(8,128)} %layer.1) | data formatting | bytes 786432
  (1 shorter events, 0.0 us)
Async XLA Ops:
  0.0 0.7 copy-start.2
  0.0 0.7 copy-start
  0.7 0.7 copy-start.1

commit v2 on v0

v2 whole, which is shorter than its diff:
```python
import jax
import jax.numpy as jnp
from jax import lax
from jax.experimental import pallas as pl
from jax.experimental.pallas import tpu as pltpu
from jax.sharding import Mesh
from jax.sharding import PartitionSpec as P

D = 6144
HD = 128
IMAGE = 256
NX, NZ = 4, 8
BLOCK = 64
ROWS = 1024
PIECE = 1536
HALF = 768
UNITS = 96
EPS = 1e-06
MESH = pl.DeviceIdType.MESH
F32, BF16 = jnp.float32, jnp.bfloat16
NT = (((1,), (1,)), ((), ()))


CHUNKS = (("z", 0, 256), ("y", 256, 512), ("z", 768, 512), ("y", 1280, 256))
N_SEMS = 320
LINK_RATE, LATENCY, ISSUE = 46.5e3, 2.3, 0.03


class Task:
    def __init__(self, name, takes=(), deps=(), work=0.02, body=None, pushes=(), prio=0.0):
        self.name, self.takes, self.deps, self.work = name, list(takes), list(deps), work
        self.body, self.pushes, self.prio = body, list(pushes), prio


def in_order(tasks):
    now, arrival, free, done, order, left = 0.0, {}, {}, set(), [], list(tasks)
    while left:
        best = None
        for task in left:
            if all(d in done for d in task.deps) and all(k in arrival for k, _ in task.takes):
                ready = max([now] + [arrival[k] for k, _ in task.takes])
                if best is None or (ready, task.prio) < best[:2]:
                    best = (ready, task.prio, task)
        now, _, task = best
        now += task.work
        for key, link, size, _ in task.pushes:
            now += ISSUE
            free[link] = max(now, free.get(link, 0.0)) + size / LINK_RATE
            arrival[key] = free[link] + LATENCY
        done.add(task.name)
        order.append(task)
        left.remove(task)
    return order


def kernel(
    tok_hbm, ln_gain, wq, wm, q_gain, k_gain, ow, bias_in, mo,
    out,
    tok, stats, stats_in, xg, WQ, WM, BV, BI, OW, MO, hp, hx, att, part, *rest,
):
    chunk_refs, (send, recv, local) = rest[:-3], rest[-3:]
    x, yl, k = lax.axis_index("x"), lax.axis_index("yl"), lax.axis_index("k")
    z, yh = lax.axis_index("z"), lax.axis_index("yh")
    nl, nk, nh = 1 - yl, 1 - k, 1 - yh
    xs = [lax.rem(x + d, NX) for d in range(NX)]
    zn = [lax.rem(z + d, NZ) for d in range(NZ)]
    at_x = lambda d: {"x": xs[d % NX]}
    at_z = lambda d: {"z": zn[d % NZ]}
    flip_l, flip_lh = {"yl": nl}, {"yl": nl, "yh": nh}
    partner, flip_lk = {"k": nk}, {"yl": nl, "k": nk}
    rel_l, rel_h = (yl, nl, nl, yl), (yh, yh, nh, nh)

    index, started = {}, []

    def push(key, src, dst, peer):
        i = index.setdefault(key, len(index))
        copy = pltpu.make_async_remote_copy(
            src_ref=src, dst_ref=dst, send_sem=send.at[i], recv_sem=recv.at[i],
            device_id=peer, device_id_type=MESH,
        )
        copy.start()
        started.append(copy)

    def take(key, dst):
        i = index.setdefault(key, len(index))
        pltpu.make_async_remote_copy(
            src_ref=dst, dst_ref=dst, send_sem=send.at[i], recv_sem=recv.at[i],
            device_id=partner, device_id_type=MESH,
        ).wait_recv()

    tok_copy = pltpu.make_async_copy(tok_hbm, tok, local.at[4])
    tok_copy.start()
    barrier = pltpu.get_barrier_semaphore()
    peers = [at_x(1), at_x(-1), at_x(2), at_z(1), at_z(-1), flip_l, flip_lh, partner, flip_lk]
    for peer in peers:
        pl.semaphore_signal(barrier, inc=1, device_id=peer, device_id_type=MESH)

    tasks = []

    def task(*args, **kwargs):
        tasks.append(Task(*args, **kwargs))

    def cols_of(w):
        return pl.ds(*CHUNKS[w[1]][1:]) if isinstance(w, tuple) else pl.ds(0, PIECE)

    def stored(w, j, c=None):
        c = cols_of(w) if c is None else c
        if w == "q":
            return wq.at[:, j, :, c]
        return {"i": wm, "o": ow, "m": mo}[w[0]].at[j, :, c]

    def gathered(w, q, s, c=None):
        c = cols_of(w) if c is None else c
        if w == "q":
            return WQ.at[q, :, s, :, c]
        return {"i": WM, "o": OW, "m": MO}[w[0]].at[q, s, :, c]

    def part_of(w, q, s, d):
        lo = 0 if d == 1 else 1
        if w in ("q", "i"):
            return gathered(w, q, s, pl.ds(lo * HALF, HALF))
        rows = 16 if w[0] == "o" else 48
        ref = OW if w[0] == "o" else MO
        return ref.at[q, s, pl.ds(lo * rows, rows), cols_of(w)]

    def bytes_of(w):
        width = CHUNKS[w[1]][2] if isinstance(w, tuple) else PIECE
        return (32 if w[0] == "o" else UNITS) * width * 2

    quarter = (yl, nl)

    def x_push(w, q):
        def refs(d):
            dst = gathered(w, quarter[q], x)
            return (stored(w, yl) if q == 0 else dst), dst, at_x(d)
        return [(("x", w, q, d), ("x", d), bytes_of(w), lambda d=d: refs(d)) for d in (1, -1)]

    def w_push(w, h=None):
        c = None if h is None else pl.ds(h * HALF, HALF)
        size = bytes_of(w) if h is None else bytes_of(w) // 2
        return (("w", w, h), "l", size, lambda: (stored(w, nl, c), gathered(w, yl, x, c), flip_l))

    def w_take(w, h=None):
        c = None if h is None else pl.ds(h * HALF, HALF)
        return (("w", w, h), lambda: gathered(w, nl, x, c))

    def x_relay(w, q, deps):
        for d in (1, -1):
            def refs(d=d):
                ref = part_of(w, quarter[q], xs[-d % NX], d)
                return ref, ref, at_x(d)
            task(
                ("x", w, q, d), deps=deps, prio=-1,
                takes=[(("x", w, q, d), lambda d=d: gathered(w, quarter[q], xs[-d % NX]))],
                pushes=[(("x2", w, q, d), ("x", d), bytes_of(w) // 2, refs)],
            )

    def x_last(w):
        return [
            (("x2", w, q, d), lambda q=q, d=d: part_of(w, quarter[q], xs[2], d))
            for q in range(2) for d in (1, -1)
        ]

    def stats_push(i, peer, link):
        return (("stats", i), link, BLOCK * 128 * 4, lambda: (stats, stats_in.at[i], peer))

    local_copies = []

    def begin():
        pl.semaphore_wait(barrier, len(peers))
        for i, w in enumerate(("q", "i")):
            copy = pltpu.make_async_copy(stored(w, yl), gathered(w, yl, x), local.at[i])
            copy.start()
            local_copies.append(copy)
        for i, (src, dst) in enumerate(((ow, OW), (mo, MO))):
            copy = pltpu.make_async_copy(src.at[yl], dst.at[yl, x], local.at[2 + i])
            copy.start()
            local_copies.append(copy)

    def statistics():
        tok_copy.wait()
        t = tok[...].astype(F32)
        s1 = jnp.sum(t, 1, keepdims=True)
        s2 = jnp.sum(t * t, 1, keepdims=True)
        lane = lax.broadcasted_iota(jnp.int32, (BLOCK, 128), 1)
        stats[...] = jnp.where(lane < 64, s1, s2)

    def bias_columns():
        b = bias_in[...].astype(F32)
        for i in range(2):
            BV[pl.ds(i * 128, 128), :] = jnp.broadcast_to(b[i : i + 1], (128, 128)).T.astype(BF16)
        mine = pl.ds(pl.multiple_of(yl * UNITS, 32), UNITS)
        BI[x] = BV[mine, :]

    def bias_refs(d):
        return BI.at[x], BI.at[x], at_x(d)

    def normalise():
        total = stats[...] + stats_in[0] + stats_in[1] + stats_in[2]
        mean = total[:, 0:1] * (1.0 / D)
        var = total[:, 64:65] * (1.0 / D) - mean * mean
        t = tok[...].astype(F32)
        g = ln_gain[...].astype(F32)
        g = jnp.concatenate([g[i : i + 1] for i in range(PIECE // 128)], axis=1)
        normed = ((t - mean) * lax.rsqrt(var + EPS) * g).astype(BF16)
        own_row = pl.multiple_of((z * 2 + yh) * BLOCK, BLOCK)
        xg[0, yl, pl.ds(own_row, BLOCK)] = normed[:, :HALF]
        xg[1, yl, pl.ds(own_row, BLOCK)] = normed[:, HALF:]

    size = BLOCK * HALF * 2

    def tokens_at(h, r, dz):
        row = pl.multiple_of((zn[dz % NZ] * 2 + rel_h[r]) * BLOCK, BLOCK)
        return xg.at[h, rel_l[r], pl.ds(row, BLOCK)]

    def z_half(ref, d):
        return ref.at[pl.ds(0 if d == 1 else BLOCK // 2, BLOCK // 2)]

    def z_ref(h, r, d, dist, back):
        ref = tokens_at(h, r, -d * (dist - back))
        return z_half(ref, d) if dist == 4 else ref

    def z_push(h, r, d, dist):
        def refs():
            ref = z_ref(h, r, d, dist, 1)
            return ref, ref, at_z(d)
        return (("z", h, r, d, dist), ("z", d), size // 2 if dist == 4 else size, refs)

    def z_take(h, r, d, dist):
        return (("z", h, r, d, dist), lambda: z_ref(h, r, d, dist, 0))

    def y_copy(kind, h, r, dz, link, peer):
        def refs():
            ref = tokens_at(h, r, dz)
            return ref, ref, peer
        return ((kind, h, dz % NZ), link, size, refs)

    def y_push(h, dz):
        return [y_copy("yl", h, 0, dz, "l", flip_l), y_copy("yn", h, 0, dz, "n", flip_lh)]

    def y_take(kind, h, dz):
        r = {"yl": 1, "yn": 2, "yr": 3}[kind]
        return ((kind, h, dz % NZ), lambda: tokens_at(h, r, dz))

    def z_first(h, r):
        return [z_push(h, r, d, 1) for d in (1, -1)]

    task(("begin",), body=begin, pushes=x_push("q", 0), work=0.0, prio=-100)
    task(
        ("stats",), deps=[("begin",)], body=statistics, work=1.0, prio=-99,
        pushes=[stats_push(0, partner, "k"), stats_push(1, flip_l, "l"), stats_push(2, flip_lk, "l")]
        + [w_push("q", 0)] + x_push("i", 0),
    )
    task(
        ("bias",), deps=[("stats",)], body=bias_columns, work=0.3, prio=-98,
        pushes=[(("bias", d), "b", 0, lambda d=d: bias_refs(d)) for d in (1, -1, 2)],
    )
    task(
        ("norm",), deps=[("bias",)], body=normalise, work=0.8, prio=-97,
        takes=[(("stats", i), lambda i=i: stats_in.at[i]) for i in range(3)],
        pushes=z_first(0, 0) + z_first(1, 0) + y_push(1, 0) + y_push(0, 0)
        + [w_push("q", 1), w_push("i", 0)],
    )
    gather = []
    for h in range(2):
        for r in range(1 if h == 0 else 4):
            for d in (1, -1):
                for dist in (1, 2, 3):
                    task(
                        ("z", h, r, d, dist), deps=[("norm",)], prio=0 if h == 0 else 5,
                        takes=[z_take(h, r, d, dist)],
                        pushes=[z_push(h, r, d, dist + 1)] + (y_push(0, -d * dist) if h == 0 else []),
                    )
    task(("z4",), takes=[z_take(0, 0, 1, 4), z_take(0, 0, -1, 4)], pushes=y_push(0, 4))
    for dz in range(NZ):
        task(
            ("yl", 0, dz), deps=[("norm",)], prio=1, takes=[y_take("yl", 0, dz)],
            pushes=[y_copy("yr", 0, 1, dz, "n", flip_lh)],
        )
    task(
        ("yl", 1, 0), deps=[("norm",)], prio=1, takes=[y_take("yl", 1, 0)],
        pushes=[y_copy("yr", 1, 1, 0, "n", flip_lh)] + z_first(1, 1),
    )
    task(("yn", 1, 0), deps=[("norm",)], prio=2, takes=[y_take("yn", 1, 0)], pushes=z_first(1, 2))
    task(("yr", 1, 0), deps=[("norm",)], prio=2, takes=[y_take("yr", 1, 0)], pushes=z_first(1, 3))
    task(("w", "i", 1), deps=[("z", 0, 0, 1, 1)], prio=3, pushes=[w_push("i", 1)])
    for w in ("q", "i"):
        task(
            ("w", w), deps=[("norm",)] + ([("w", "i", 1)] if w == "i" else []), prio=2,
            takes=[w_take(w, 0), w_take(w, 1)], pushes=x_push(w, 1),
        )
        x_relay(w, 0, [("norm",)])
        x_relay(w, 1, [("w", w)])
    n = len(CHUNKS)
    for c in range(n):
        pair = (("o", c), ("m", c))
        if c == 0:
            after = [("z", 0, 0, 1, 3), ("z", 0, 0, -1, 3)]
        else:
            after = [("w2s", c - 1)] + ([("w2p", c - 2)] if c >= 2 else [])
        task(("w2s", c), deps=after, prio=6, pushes=[w_push(w) for w in pair])
        if c == 0:
            after = [("x", "i", 0, 1), ("x", "i", 0, -1), ("w", "i"), ("x", "q", 1, 1), ("x", "q", 1, -1)]
        else:
            after = [("w2q", c - 1)] + ([("x", "i", 1, 1), ("x", "i", 1, -1)] if c == 1 else [])
        task(("w2p", c), deps=after, prio=7, pushes=x_push(pair[0], 0) + x_push(pair[1], 0))
        task(
            ("w2q", c), deps=[("w2s", c), ("w2p", c)], prio=7, takes=[w_take(w) for w in pair],
            pushes=x_push(pair[0], 1) + x_push(pair[1], 1),
        )
        for w in pair:
            x_relay(w, 0, [("w2p", c)])
            x_relay(w, 1, [("w2q", c)])
    first_relays = [t.name for t in tasks if t.name[0] in ("z", "z4", "yl", "yn", "yr", "w")]
    first_relays += [("x", w, q, d) for w in ("q", "i") for q in range(2) for d in (1, -1)]

    def project(i):
        row = pl.multiple_of(lax.rem(i * 256 + nk * 512, ROWS), 256)
        acc_q = jnp.zeros((256, 384), F32)
        acc_m = jnp.zeros((256, 384), F32)
        for q in range(2):
            for h in range(2):
                lhs = xg[h, q, pl.ds(row, 256)]
                cols = slice(h * HALF, (h + 1) * HALF)
                acc_q += lax.dot_general(
                    lhs, WQ[q, :, :, :, cols].reshape(384, HALF), NT, preferred_element_type=F32
                )
                acc_m += lax.dot_general(
                    lhs, WM[q, :, :, cols].reshape(384, HALF), NT, preferred_element_type=F32
                )
        hp[pl.ds(row, 256), pl.ds(0, 384)] = acc_q
        hp[pl.ds(row, 256), pl.ds(384, 384)] = acc_m

    def project_first():
        for copy in local_copies[:2]:
            copy.wait()
        project(0)

    def hx_refs(i):
        theirs = hp.at[pl.ds(pl.multiple_of(nk * 512 + i * 256, 256), 256)]
        return theirs, hx.at[pl.ds(i * 256, 256)], partner

    all_in = x_last("q") + x_last("i")
    all_in += [y_take(kind, 0, dz) for dz in range(NZ) for kind in ("yn", "yr")]
    all_in += [z_take(1, r, d, 4) for r in range(4) for d in (1, -1)]
    k_scale = LINK_RATE / 600e3
    for i in range(4):
        task(
            ("p", i), takes=all_in if i == 0 else [], deps=first_relays if i == 0 else [("p", i - 1)],
            body=project_first if i == 0 else (lambda i=i: project(i)), work=1.8, prio=10,
            pushes=[(("hx", i), "k", 256 * HALF * 4 * k_scale, lambda i=i: hx_refs(i))] if i < 2 else [],
        )

    def head_norm(values, gain):
        centred = values - jnp.mean(values, -1, keepdims=True)
        spread = jnp.mean(centred * centred, -1, keepdims=True)
        return (centred * lax.rsqrt(spread + EPS) * gain[...].astype(F32)).astype(BF16)

    def image(i):
        mine = pl.ds(i * IMAGE, IMAGE)
        row = pl.multiple_of(k * 512 + i * IMAGE, IMAGE)
        joined = hp[pl.ds(row, IMAGE)] + hx[mine]
        q = head_norm(joined[:, 0:128], q_gain)
        kk = head_norm(joined[:, 128:256], k_gain)
        v = joined[:, 256:384].astype(BF16)
        scores = lax.dot_general(q, kk, NT, preferred_element_type=F32) * HD ** (-0.5)
        e = jnp.exp(scores - jnp.max(scores, -1, keepdims=True))
        probs = (e / jnp.sum(e, -1, keepdims=True)).astype(BF16)
        attended = jnp.dot(probs, v, preferred_element_type=F32)
        att[k, mine, pl.ds(0, 128)] = attended.astype(BF16)
        unit = (lax.broadcasted_iota(jnp.int32, (IMAGE, 128), 1) == 0).astype(F32).astype(BF16)
        pre = joined[:, 384:768] + lax.dot_general(
            unit, BI[...].reshape(384, 128), NT, preferred_element_type=F32
        )
        hidden = 0.5 * pre * (1.0 + lax.erf(pre * (0.5 ** 0.5)))
        att[k, mine, pl.ds(128, 384)] = hidden.astype(BF16)

    def att_refs(i):
        ref = att.at[k, pl.ds(i * IMAGE, IMAGE)]
        return ref, ref, partner

    for i in range(2):
        takes = [(("hx", i), lambda i=i: hx.at[pl.ds(i * 256, 256)])]
        if i == 0:
            takes += [(("bias", d), lambda d=d: BI.at[xs[-d % NX]]) for d in (1, -1, 2)]
        task(
            ("image", i), takes=takes, deps=[("p", 3)] + [("image", 0)] * i, prio=10, work=0.8,
            body=lambda i=i: image(i),
            pushes=[(("att", i), "k", 256 * 512 * 2 * k_scale, lambda i=i: att_refs(i))],
        )

    def output_terms(c, half):
        if c == 0 and half == 0:
            for copy in local_copies[2:]:
                copy.wait()
        _, c0, width = CHUNKS[c]
        who = k if half == 0 else nk
        cols = slice(c0, c0 + width)
        for i in range(2):
            row = pl.multiple_of(who * 512 + i * 256, 256)
            a = att[who, pl.ds(i * 256, 256)]
            for q in range(2):
                part[q, pl.ds(row, 256), pl.ds(c0, width)] = jnp.dot(
                    a[:, :128], OW[q, :, :, cols].reshape(128, width), preferred_element_type=F32
                ) + jnp.dot(
                    a[:, 128:], MO[q, :, :, cols].reshape(384, width), preferred_element_type=F32
                )

    for c, (_, _, width) in enumerate(CHUNKS):
        pair = (("o", c), ("m", c))
        for half in range(2):
            deps = [("image", 1)]
            deps += [("x", w, q, d) for w in pair for q in range(2) for d in (1, -1)]
            deps += [("terms", c, 0)] if half else []
            deps += [("terms", c - 1, 1)] if c else []
            takes = (x_last(pair[0]) + x_last(pair[1])) if half == 0 else []
            if c == 0 and half == 1:
                takes = [
                    (("att", i), lambda i=i: att.at[nk, pl.ds(i * IMAGE, IMAGE)]) for i in range(2)
                ]
            task(
                ("terms", c, half), takes=takes, deps=deps, prio=9, work=1.44 * width / 768,
                body=lambda c=c, half=half: output_terms(c, half),
            )

    half = BLOCK // 2

    def term(c, r, dz):
        row = pl.multiple_of((zn[dz % NZ] * 2 + rel_h[r]) * BLOCK, BLOCK)
        return part.at[rel_l[r], pl.ds(row, BLOCK), pl.ds(*CHUNKS[c][1:])]

    def reduction(c):
        kind, _, width = CHUNKS[c]
        zs, zr, ns, nr, ms, mr = chunk_refs[6 * c : 6 * c + 6]
        block, groups = BLOCK * width * 2, (1 if kind == "y" else 4)
        work = 0.05 + 0.12 * width / HALF
        ready = ("terms", c, 1)

        def along_z(g, r, d, dist):
            slot, landing = zs.at[g, 0 if d == 1 else 1, dist - 1], zr.at[g, 0 if d == 1 else 1, dist - 1]
            if dist == 4:
                slot, landing = slot.at[pl.ds(0, half)], landing.at[pl.ds(0, half)]
            before = zr.at[g, 0 if d == 1 else 1, min(dist, 3)]
            if dist == 3:
                before = before.at[pl.ds(0, half)]
            lo = 0 if d == 1 else half

            def body():
                blk = term(c, r, d * dist)
                if dist == 4:
                    slot[...] = blk[pl.ds(lo, half)].astype(BF16)
                elif dist == 3:
                    slot[pl.ds(half - lo, half)] = blk[pl.ds(half - lo, half)].astype(BF16)
                    slot[pl.ds(lo, half)] = (
                        blk[pl.ds(lo, half)] + before[...].astype(F32)
                    ).astype(BF16)
                else:
                    slot[...] = (blk[...] + before[...].astype(F32)).astype(BF16)

            from_y = ("y_end", c, (d * dist) % NZ) if kind == "y" else ready
            prio = 3 if kind == "y" else 8 - dist * 0.5 + (0 if r in (2, 3) else 0.3)
            task(
                ("c", c, r, d, dist), body=body, work=work, prio=prio + c * 0.01,
                takes=[] if dist == 4 else [(("c", c, r, d, dist + 1), lambda: before)],
                deps=[from_y] + ([] if dist == 4 else [("c", c, r, d, dist + 1)]),
                pushes=[
                    (("c", c, r, d, dist), ("z", d), block // 2 if dist == 4 else block,
                     lambda: (slot, landing, at_z(d)))
                ],
            )

        def z_end(g, r):
            def body():
                blk = term(c, r, 0)
                blk[...] = blk[...] + zr[g, 0, 0].astype(F32) + zr[g, 1, 0].astype(F32)
            task(
                ("z_end", c, r), body=body, work=work, prio=2,
                takes=[(("c", c, r, d, 1), lambda i=i: zr.at[g, i, 0]) for i, d in enumerate((1, -1))],
                deps=[("c", c, r, d, 1) for d in (1, -1)] + ([("y_end", c, 0)] if kind == "y" else []),
            )

        def along_y(g, dz, deps_out, deps_mid, deps_end, prios):
            tree = (c + dz) % 2
            far, near = ((flip_lh, "n"), (flip_l, "l")) if tree == 0 else ((flip_l, "l"), (flip_lh, "n"))
            direct, mid = (2, 1) if tree == 0 else (1, 2)

            def out_body():
                for j, r in enumerate((direct, 3)):
                    ns[g, j] = term(c, r, dz)[...].astype(BF16)

            def mid_body():
                ms[g] = (term(c, mid, dz)[...] + nr[g, 1].astype(F32)).astype(BF16)

            def end_body():
                blk = term(c, 0, dz)
                blk[...] = blk[...] + nr[g, 0].astype(F32) + mr[g].astype(F32)

            task(
                ("y_out", c, dz), body=out_body, deps=deps_out(direct), prio=prios[0],
                work=0.05 + 0.15 * width / HALF,
                pushes=[
                    (("n", c, dz, j), far[1], block, lambda j=j: (ns.at[g, j], nr.at[g, j], far[0]))
                    for j in (1, 0)
                ],
            )
            task(
                ("y_mid", c, dz), body=mid_body, work=work, prio=prios[1],
                takes=[(("n", c, dz, 1), lambda: nr.at[g, 1])],
                deps=[("y_out", c, dz)] + deps_mid(mid),
                pushes=[(("m", c, dz), near[1], block, lambda: (ms.at[g], mr.at[g], near[0]))],
            )
            task(
                ("y_end", c, dz), body=end_body, work=work, prio=prios[2],
                takes=[(("n", c, dz, 0), lambda: nr.at[g, 0]), (("m", c, dz), lambda: mr.at[g])],
                deps=[("y_mid", c, dz)] + deps_end,
            )

        if kind == "y":
            for dz in range(NZ):
                far = min(dz, NZ - dz)
                along_y(
                    dz, dz, lambda r: [ready], lambda r: [], [],
                    (20 - far, 4 - far * 0.1, 5 - far * 0.1),
                )
        for g in range(groups):
            for d in (1, -1):
                for dist in (4, 3, 2, 1):
                    along_z(g, g, d, dist)
            z_end(g, g)
        if kind == "z":
            along_y(
                0, 0, lambda r: [("z_end", c, r), ("z_end", c, 3)], lambda r: [("z_end", c, r)],
                [("z_end", c, 0)], (1, 1, 1),
            )

    for c in range(n):
        reduction(c)

    for step in in_order(tasks):
        for key, ref in step.takes:
            take(key, ref())
        if step.body is not None:
            step.body()
        for key, _, _, refs in step.pushes:
            push(key, *refs())

    own = pl.ds(pl.multiple_of((z * 2 + yh) * BLOCK, BLOCK), BLOCK)
    out[...] = part[yl, own]
    for copy in started:
        copy.wait_send()
    assert len(index) <= N_SEMS, len(index)


def per_device(
    tokens, ln_gain, qkv_weight, q_gain, k_gain, out_weight, mlp_in, mlp_bias, mlp_out, out_bias
):
    wq = jnp.transpose(qkv_weight, (1, 2, 3, 0))
    wm = jnp.transpose(mlp_in).reshape(2, UNITS, PIECE)
    mo = mlp_out.reshape(2, UNITS, PIECE)
    bias = jnp.pad(mlp_bias, (0, 64)).reshape(2, 128)
    vm, hbm = pl.BlockSpec(memory_space=pltpu.VMEM), pl.BlockSpec(memory_space=pl.ANY)
    scratch = [
        pltpu.VMEM((BLOCK, PIECE), BF16),
        pltpu.VMEM((BLOCK, 128), F32),
        pltpu.VMEM((3, BLOCK, 128), F32),
        pltpu.VMEM((2, 2, ROWS, HALF), BF16),
        pltpu.VMEM((2, 3, NX, 32, PIECE), BF16),
        pltpu.VMEM((2, NX, UNITS, PIECE), BF16),
        pltpu.VMEM((256, 128), BF16),
        pltpu.VMEM((NX, UNITS, 128), BF16),
        pltpu.VMEM((2, NX, 32, PIECE), BF16),
        pltpu.VMEM((2, NX, UNITS, PIECE), BF16),
        pltpu.VMEM((ROWS, HALF), F32),
        pltpu.VMEM((512, HALF), F32),
        pltpu.VMEM((2, 512, 512), BF16),
        pltpu.VMEM((2, ROWS, PIECE), F32),
    ]
    for kind, _, width in CHUNKS:
        block = (BLOCK, width)
        groups, ys = (1, NZ) if kind == "y" else (4, 1)
        scratch += [pltpu.VMEM((groups, 2, 4, *block), BF16)] * 2
        scratch += [pltpu.VMEM((ys, 2, *block), BF16)] * 2
        scratch += [pltpu.VMEM((ys, *block), BF16)] * 2
    scratch += [
        pltpu.SemaphoreType.DMA((N_SEMS,)),
        pltpu.SemaphoreType.DMA((N_SEMS,)),
        pltpu.SemaphoreType.DMA((5,)),
    ]
    sums = pl.pallas_call(
        kernel,
        out_shape=jax.ShapeDtypeStruct((BLOCK, PIECE), F32),
        in_specs=[hbm, vm, hbm, hbm, vm, vm, hbm, vm, hbm],
        out_specs=vm,
        scratch_shapes=scratch,
        compiler_params=pltpu.CompilerParams(
            collective_id=0, has_side_effects=True, vmem_limit_bytes=60 * 1024 * 1024
        ),
        name="layer",
    )(
        tokens, ln_gain.reshape(PIECE // 128, 128), wq, wm, q_gain.reshape(1, HD),
        k_gain.reshape(1, HD), out_weight, bias, mo,
    )
    return tokens.astype(F32) + sums + out_bias.astype(F32)


def solution(mesh):
    split = Mesh(
        mesh.devices.reshape(NX, 2, 2, NZ, 2), ("x", "yl", "k", "z", "yh")
    )
    token_axes, row, col = ("x", "z", "yh"), ("yl", "k"), ("z", "yh")
    placed = (
        P(token_axes, row),
        P(row),
        P(row, None, col, "x"),
        P(),
        P(),
        P(col, "x", row),
        P(row, token_axes),
        P(token_axes),
        P(token_axes, row),
        P(row),
    )
    return jax.shard_map(
        per_device, mesh=split, in_specs=placed, out_specs=P(token_axes, row), check_vma=False
    )
```

time: 342 us -> 127 us (0.37)
  waiting for transfers between devices: 255 us -> 0 us
  Pallas kernels: 0 us -> 124 us
  matrix products: 19.6 us -> 0 us
  starting transfers between devices: 15.3 us -> 0 us
  blocking collectives: 14.2 us -> 0 us
  between operations: 13.6 us -> 0.03 us
  other arithmetic: 15 us -> 1.79 us
  local copies, waits for them, and re-layouts: 7.4 us -> 1.18 us
    reduce_scatter x3 -> x0, waiting for transfers between devices: 138 us -> none  [the longest x2 71 us: own_rows(): total = lax.psum_scatter(total, axis, scatter_dimension=0, tiled=True)]
    pallas_call x0 -> x1, Pallas kernels: none -> 124 us  [per_device(): pl.pallas_call(kernel, out_shape=jax.ShapeDtypeStruct((BLOCK, PIECE), F32...]
    all_gather x3 -> x0, waiting for transfers between devices: 87 us -> none  [the longest x1 49.6 us: per_device(): normed_all = lax.all_gather(normed, COL, axis=0, tiled=True)]
    all_to_all x3 -> x0, waiting for transfers between devices: 29.9 us -> none  [copy_for_each(): return lax.all_to_all(copies, axis, split_axis=0, concat_axis=0, tiled=True)]
    dot_general x6 -> x0, matrix products: 19.6 us -> none  [the longest x1 5.25 us: per_device(): jnp.dot(normed_all, gather_directly(mlp_in, 'store', 1), preferred_elemen...]
    all_to_all x3 -> x0, starting transfers between devices: 15.1 us -> none  [copy_for_each(): return lax.all_to_all(copies, axis, split_axis=0, concat_axis=0, tiled=True)]
    all_gather x1 -> x0, blocking collectives: 14.2 us -> none  [per_device(): lax.all_gather(out_weight, 'store', axis=1, tiled=True)]
    concatenate x4 -> x0, other arithmetic: 5.06 us -> none  [the longest x1 3.26 us: in_one_piece(): both = jnp.concatenate(arrays, axis=along)]
  transfers between devices with their start and end apart: 9 -> 0, of which waited for: 8 -> 0; matrix products, arithmetic and copies ran while one was open for 7% -> 0% of each run, Pallas kernels for 0% -> 0%
where the time goes in v2:
time: 127 us
  Pallas kernels  124 us (98%)
  other arithmetic  1.79 us (1%)
    pallas_call x1, Pallas kernels, per_device(): pl.pallas_call(kernel, out_shape=jax.ShapeDtypeStruct((BLOCK, PIECE), F32...  124 us

profile of v2, /device:TPU:2, one launch (start us, length us, event | category | flops | bytes accessed | tf_op | source)
XLA Modules:
  0.0 126.7 jit_solution(18372360166555534839)
XLA Ops:
  0.0 1.2 pad_bitcast_fusion.bias_in
  1.2 0.0 copy-start.1
  1.2 0.0 copy-start
  1.2 123.7 %layer.1 = f32[64,1536]{1,0:T(8,128)} custom-call(bf16[64,1536]{1,0:T(8,128)(2,1)} %tok_hbm.1, bf16[12,128]{1,0:T(8,128)(2,1)} %bitcast.13, bf16[3,2,32,1536]{3,2,1,0:T(8,128)(2,1)} %bitcast.10, bf16[2,96,1536]{2,1,0:T(8,128)(2,1)} %bitcast.11, bf16[1,128]{1,0:T(2,128)(2,1)} %bitcast.14, bf16[1,128]{1,0:T(2,128)(2,1)} %bitcast.15, bf16[2,32,1536]{2,1,0:T(8,128)(2,1)} %ow.1, ...), custom_call_target="tpu_custom_call" | custom-call | tf_op jit(solution)/shard_map/layer/pallas_call | solution.py:589
  124.8 0.0 copy-done.1
  124.9 0.0 copy-done
  124.9 1.8 %add_add_fusion = f32[64,1536]{1,0:T(8,128)} fusion(f32[64,1536]{1,0:T(8,128)} %layer.1, bf16[64,1536]{1,0:T(8,128)(2,1)S(1)} %copy-done, f32[1536]{0:T(1024)S(1)} %convert_element_type.9), kind=kLoop, calls=%fused_computation | loop fusion | flops 294912 | bytes 989184 | tf_op jit(solution)/shard_map/add | solution.py:603
  (1 shorter events, 0.0 us)
Async XLA Ops:
  1.2 123.7 %copy-start.1 = (bf16[1536]{0:T(1024)(128)(2,1)S(1)}, bf16[1536]{0:T(1024)(128)(2,1)}, u32[]{:S(2)}) copy-start(bf16[1536]{0:T(1024)(128)(2,1)} %param.19) | copy-start | bytes 9220
  1.2 123.7 %copy-start = (bf16[64,1536]{1,0:T(8,128)(2,1)S(1)}, bf16[64,1536]{1,0:T(8,128)(2,1)}, u32[]{:S(2)}) copy-start(bf16[64,1536]{1,0:T(8,128)(2,1)} %tok_hbm.1) | copy-start | bytes 589828

commit v3 on v2

--- a/solution.py
+++ b/solution.py
@@ -23,7 +23,7 @@
 
 CHUNKS = (("z", 0, 256), ("y", 256, 512), ("z", 768, 512), ("y", 1280, 256))
 N_SEMS = 320
-LINK_RATE, LATENCY, ISSUE = 46.5e3, 2.3, 0.03
+LINK_RATE, LATENCY, ISSUE = 44e3, 2.3, 0.03
 
 
 class Task:
@@ -56,7 +56,7 @@
 def kernel(
     tok_hbm, ln_gain, wq, wm, q_gain, k_gain, ow, bias_in, mo,
     out,
-    tok, stats, stats_in, xg, WQ, WM, BV, BI, OW, MO, hp, hx, att, part, *rest,
+    tok, stats, stats_in, xg, WQ, WM, BV, BI, OW, MO, hq, hm, hxq, hxm, att, part, *rest,
 ):
     chunk_refs, (send, recv, local) = rest[:-3], rest[-3:]
     x, yl, k = lax.axis_index("x"), lax.axis_index("yl"), lax.axis_index("k")
@@ -162,7 +162,7 @@
         ]
 
     def stats_push(i, peer, link):
-        return (("stats", i), link, BLOCK * 128 * 4, lambda: (stats, stats_in.at[i], peer))
+        return (("stats", i), link, 8 * 128 * 4, lambda: (stats, stats_in.at[i], peer))
 
     local_copies = []
 
@@ -183,7 +183,10 @@
         s1 = jnp.sum(t, 1, keepdims=True)
         s2 = jnp.sum(t * t, 1, keepdims=True)
         lane = lax.broadcasted_iota(jnp.int32, (BLOCK, 128), 1)
-        stats[...] = jnp.where(lane < 64, s1, s2)
+        both = jnp.where(lane < 64, s1, s2)
+        turned = jnp.concatenate([both, both], axis=0).T
+        row = lax.broadcasted_iota(jnp.int32, (8, 128), 0)
+        stats[...] = jnp.where(row < 4, turned[0:1], turned[64:65])
 
     def bias_columns():
         b = bias_in[...].astype(F32)
@@ -197,12 +200,15 @@
 
     def normalise():
         total = stats[...] + stats_in[0] + stats_in[1] + stats_in[2]
-        mean = total[:, 0:1] * (1.0 / D)
-        var = total[:, 64:65] * (1.0 / D) - mean * mean
+        mean = total[0:1] * (1.0 / D)
+        var = total[4:5] * (1.0 / D) - mean * mean
+        row = lax.broadcasted_iota(jnp.int32, (128, 128), 0)
+        turned = jnp.where(row < 64, mean, lax.rsqrt(var + EPS)).T
+        mean, scale = turned[:BLOCK, 0:1], turned[:BLOCK, 64:65]
         t = tok[...].astype(F32)
         g = ln_gain[...].astype(F32)
         g = jnp.concatenate([g[i : i + 1] for i in range(PIECE // 128)], axis=1)
-        normed = ((t - mean) * lax.rsqrt(var + EPS) * g).astype(BF16)
+        normed = ((t - mean) * scale * g).astype(BF16)
         own_row = pl.multiple_of((z * 2 + yh) * BLOCK, BLOCK)
         xg[0, yl, pl.ds(own_row, BLOCK)] = normed[:, :HALF]
         xg[1, yl, pl.ds(own_row, BLOCK)] = normed[:, HALF:]
@@ -314,41 +320,76 @@
     first_relays = [t.name for t in tasks if t.name[0] in ("z", "z4", "yl", "yn", "yr", "w")]
     first_relays += [("x", w, q, d) for w in ("q", "i") for q in range(2) for d in (1, -1)]
 
-    def project(i):
-        row = pl.multiple_of(lax.rem(i * 256 + nk * 512, ROWS), 256)
-        acc_q = jnp.zeros((256, 384), F32)
-        acc_m = jnp.zeros((256, 384), F32)
-        for q in range(2):
-            for h in range(2):
-                lhs = xg[h, q, pl.ds(row, 256)]
-                cols = slice(h * HALF, (h + 1) * HALF)
-                acc_q += lax.dot_general(
-                    lhs, WQ[q, :, :, :, cols].reshape(384, HALF), NT, preferred_element_type=F32
-                )
-                acc_m += lax.dot_general(
-                    lhs, WM[q, :, :, cols].reshape(384, HALF), NT, preferred_element_type=F32
-                )
-        hp[pl.ds(row, 256), pl.ds(0, 384)] = acc_q
-        hp[pl.ds(row, 256), pl.ds(384, 384)] = acc_m
-
-    def project_first():
-        for copy in local_copies[:2]:
-            copy.wait()
-        project(0)
-
-    def hx_refs(i):
-        theirs = hp.at[pl.ds(pl.multiple_of(nk * 512 + i * 256, 256), 256)]
-        return theirs, hx.at[pl.ds(i * 256, 256)], partner
-
-    all_in = x_last("q") + x_last("i")
-    all_in += [y_take(kind, 0, dz) for dz in range(NZ) for kind in ("yn", "yr")]
-    all_in += [z_take(1, r, d, 4) for r in range(4) for d in (1, -1)]
+    groups = ((0,), (1, -1), (2, -2), (3, -3), (4,))
+
+    def rows_of(dzs):
+        return [pl.ds(pl.multiple_of(zn[dz % NZ] * 128, 128), 128) for dz in dzs]
+
+    def product(lhs, weights, h):
+        cols = pl.ds(h * HALF, HALF)
+        rhs = weights[..., cols].reshape(384, HALF)
+        return lax.dot_general(lhs, rhs, NT, preferred_element_type=F32)
+
+    def project(dzs):
+        if dzs == (0,):
+            for copy in local_copies[:2]:
+                copy.wait()
+        rows = rows_of(dzs)
+        acc_q = jnp.zeros((128 * len(dzs), 384), F32)
+        acc_m = jnp.zeros((128 * len(dzs), 384), F32)
+        for h in range(2):
+            for q in (yl, nl):
+                lhs = jnp.concatenate([xg[h, q, r] for r in rows], axis=0)
+                acc_q += product(lhs, WQ.at[q], h)
+                if q is yl:
+                    acc_m += product(lhs, WM.at[q], h)
+        for i, r in enumerate(rows):
+            hq[r] = acc_q[i * 128 : (i + 1) * 128]
+            hm[r] = acc_m[i * 128 : (i + 1) * 128]
+
+    def project_last(i):
+        row = pl.ds(pl.multiple_of(lax.rem(i * 256 + nk * 512, ROWS), 256), 256)
+        acc = hm[row]
+        for h in range(2):
+            acc += product(xg[h, nl, row], WM.at[nl], h)
+        hm[row] = acc
+
+    def hq_refs():
+        return hq.at[pl.ds(pl.multiple_of(nk * 512, 512), 512)], hxq, partner
+
+    def hm_refs(i):
+        theirs = hm.at[pl.ds(pl.multiple_of(nk * 512 + i * 256, 256), 256)]
+        return theirs, hxm.at[pl.ds(i * 256, 256)], partner
+
     k_scale = LINK_RATE / 600e3
+    early = x_last("q") + [t for t in x_last("i") if t[0][2] == 0]
+    late = [t for t in x_last("i") if t[0][2] == 1]
+    early_relays = [("x", w, q, d) for w, q in (("q", 0), ("q", 1), ("i", 0)) for d in (1, -1)]
+    late_relays = first_relays
+    for g, dzs in enumerate(groups):
+        takes, deps = (list(early), list(early_relays)) if g == 0 else ([], [("p", g - 1)])
+        for dz in dzs:
+            takes += [y_take(kind, 0, dz) for kind in ("yn", "yr")]
+            deps += [("yl", 0, dz % NZ)]
+            if dz == 0:
+                deps += [("norm",), ("yl", 1, 0), ("yn", 1, 0), ("yr", 1, 0)]
+            elif dz == 4:
+                deps += [("z4",)]
+                takes += [z_take(1, r, d, 4) for r in range(4) for d in (1, -1)]
+            else:
+                d = -1 if dz > 0 else 1
+                deps += [("z", 0, 0, d, abs(dz))] + [("z", 1, r, d, abs(dz)) for r in range(4)]
+        task(
+            ("p", g), takes=takes, deps=deps, body=lambda dzs=dzs: project(dzs), prio=30,
+            work=0.9 if len(dzs) == 1 else 1.4,
+            pushes=[(("hq",), "k", 512 * 384 * 4 * k_scale, hq_refs)] if g == 4 else [],
+        )
     for i in range(4):
         task(
-            ("p", i), takes=all_in if i == 0 else [], deps=first_relays if i == 0 else [("p", i - 1)],
-            body=project_first if i == 0 else (lambda i=i: project(i)), work=1.8, prio=10,
-            pushes=[(("hx", i), "k", 256 * HALF * 4 * k_scale, lambda i=i: hx_refs(i))] if i < 2 else [],
+            ("pl", i), takes=late if i == 0 else [],
+            deps=late_relays + [("p", 4)] if i == 0 else [("pl", i - 1)],
+            body=lambda i=i: project_last(i), work=0.5, prio=10,
+            pushes=[(("hm", i), "k", 256 * 384 * 4 * k_scale, lambda i=i: hm_refs(i))] if i < 2 else [],
         )
 
     def head_norm(values, gain):
@@ -356,10 +397,12 @@
         spread = jnp.mean(centred * centred, -1, keepdims=True)
         return (centred * lax.rsqrt(spread + EPS) * gain[...].astype(F32)).astype(BF16)
 
-    def image(i):
+    def own_rows(i):
+        return pl.ds(pl.multiple_of(k * 512 + i * IMAGE, IMAGE), IMAGE)
+
+    def attend(i):
         mine = pl.ds(i * IMAGE, IMAGE)
-        row = pl.multiple_of(k * 512 + i * IMAGE, IMAGE)
-        joined = hp[pl.ds(row, IMAGE)] + hx[mine]
+        joined = hq[own_rows(i)] + hxq[mine]
         q = head_norm(joined[:, 0:128], q_gain)
         kk = head_norm(joined[:, 128:256], k_gain)
         v = joined[:, 256:384].astype(BF16)
@@ -368,8 +411,11 @@
         probs = (e / jnp.sum(e, -1, keepdims=True)).astype(BF16)
         attended = jnp.dot(probs, v, preferred_element_type=F32)
         att[k, mine, pl.ds(0, 128)] = attended.astype(BF16)
+
+    def activate(i):
+        mine = pl.ds(i * IMAGE, IMAGE)
         unit = (lax.broadcasted_iota(jnp.int32, (IMAGE, 128), 1) == 0).astype(F32).astype(BF16)
-        pre = joined[:, 384:768] + lax.dot_general(
+        pre = hm[own_rows(i)] + hxm[mine] + lax.dot_general(
             unit, BI[...].reshape(384, 128), NT, preferred_element_type=F32
         )
         hidden = 0.5 * pre * (1.0 + lax.erf(pre * (0.5 ** 0.5)))
@@ -380,12 +426,17 @@
         return ref, ref, partner
 
     for i in range(2):
-        takes = [(("hx", i), lambda i=i: hx.at[pl.ds(i * 256, 256)])]
+        task(
+            ("attend", i), deps=[("pl", 3)] + [("attend", 0)] * i, prio=10, work=0.45,
+            takes=[(("hq",), lambda: hxq)] if i == 0 else [], body=lambda i=i: attend(i),
+        )
+    for i in range(2):
+        takes = [(("hm", i), lambda i=i: hxm.at[pl.ds(i * 256, 256)])]
         if i == 0:
             takes += [(("bias", d), lambda d=d: BI.at[xs[-d % NX]]) for d in (1, -1, 2)]
         task(
-            ("image", i), takes=takes, deps=[("p", 3)] + [("image", 0)] * i, prio=10, work=0.8,
-            body=lambda i=i: image(i),
+            ("image", i), takes=takes, deps=[("attend", 1)] + [("image", 0)] * i, prio=10, work=0.45,
+            body=lambda i=i: activate(i),
             pushes=[(("att", i), "k", 256 * 512 * 2 * k_scale, lambda i=i: att_refs(i))],
         )
 
@@ -561,8 +612,8 @@
     vm, hbm = pl.BlockSpec(memory_space=pltpu.VMEM), pl.BlockSpec(memory_space=pl.ANY)
     scratch = [
         pltpu.VMEM((BLOCK, PIECE), BF16),
-        pltpu.VMEM((BLOCK, 128), F32),
-        pltpu.VMEM((3, BLOCK, 128), F32),
+        pltpu.VMEM((8, 128), F32),
+        pltpu.VMEM((3, 8, 128), F32),
         pltpu.VMEM((2, 2, ROWS, HALF), BF16),
         pltpu.VMEM((2, 3, NX, 32, PIECE), BF16),
         pltpu.VMEM((2, NX, UNITS, PIECE), BF16),
@@ -570,8 +621,10 @@
         pltpu.VMEM((NX, UNITS, 128), BF16),
         pltpu.VMEM((2, NX, 32, PIECE), BF16),
         pltpu.VMEM((2, NX, UNITS, PIECE), BF16),
-        pltpu.VMEM((ROWS, HALF), F32),
-        pltpu.VMEM((512, HALF), F32),
+        pltpu.VMEM((ROWS, 384), F32),
+        pltpu.VMEM((ROWS, 384), F32),
+        pltpu.VMEM((512, 384), F32),
+        pltpu.VMEM((512, 384), F32),
         pltpu.VMEM((2, 512, 512), BF16),
         pltpu.VMEM((2, ROWS, PIECE), F32),
     ]

time: 127 us -> 123 us (0.969)
  Pallas kernels: 124 us -> 119 us
    pallas_call x1, Pallas kernels: 124 us -> 119 us  [per_device(): pl.pallas_call(kernel, out_shape=jax.ShapeDtypeStruct((BLOCK, PIECE), F32...]
where the time goes in v3:
time: 123 us; the launch traced here: 122 us
  Pallas kernels  119 us (97%)
  other arithmetic  1.79 us (1%)
    pallas_call x1, Pallas kernels, per_device(): pl.pallas_call(kernel, out_shape=jax.ShapeDtypeStruct((BLOCK, PIECE), F32...  119 us

profile of v3, /device:TPU:2, one launch (start us, length us, event | category | flops | bytes accessed | tf_op | source)
XLA Modules:
  0.0 122.2 jit_solution(10578625227268687621)
XLA Ops:
  0.0 1.2 pad_bitcast_fusion.bias_in
  1.2 0.0 copy-start.1
  1.2 0.0 copy-start
  1.2 119.2 %layer.1 = f32[64,1536]{1,0:T(8,128)} custom-call(bf16[64,1536]{1,0:T(8,128)(2,1)} %tok_hbm.1, bf16[12,128]{1,0:T(8,128)(2,1)} %bitcast.13, bf16[3,2,32,1536]{3,2,1,0:T(8,128)(2,1)} %bitcast.10, bf16[2,96,1536]{2,1,0:T(8,128)(2,1)} %bitcast.11, bf16[1,128]{1,0:T(2,128)(2,1)} %bitcast.14, bf16[1,128]{1,0:T(2,128)(2,1)} %bitcast.15, bf16[2,32,1536]{2,1,0:T(8,128)(2,1)} %ow.1, ...), custom_call_target="tpu_custom_call" | custom-call | tf_op jit(solution)/shard_map/layer/pallas_call | solution.py:642
  120.4 0.0 copy-done.1
  120.4 0.0 copy-done
  120.5 1.8 %add_add_fusion = f32[64,1536]{1,0:T(8,128)} fusion(f32[64,1536]{1,0:T(8,128)} %layer.1, bf16[64,1536]{1,0:T(8,128)(2,1)S(1)} %copy-done, f32[1536]{0:T(1024)S(1)} %convert_element_type.9), kind=kLoop, calls=%fused_computation | loop fusion | flops 294912 | bytes 989184 | tf_op jit(solution)/shard_map/add | solution.py:656
  (1 shorter events, 0.0 us)
Async XLA Ops:
  1.2 119.3 %copy-start.1 = (bf16[1536]{0:T(1024)(128)(2,1)S(1)}, bf16[1536]{0:T(1024)(128)(2,1)}, u32[]{:S(2)}) copy-start(bf16[1536]{0:T(1024)(128)(2,1)} %param.19) | copy-start | bytes 9220
  1.2 119.3 %copy-start = (bf16[64,1536]{1,0:T(8,128)(2,1)S(1)}, bf16[64,1536]{1,0:T(8,128)(2,1)}, u32[]{:S(2)}) copy-start(bf16[64,1536]{1,0:T(8,128)(2,1)} %tok_hbm.1) | copy-start | bytes 589828

commit v4 on v3

--- a/solution.py
+++ b/solution.py
@@ -21,9 +21,27 @@
 NT = (((1,), (1,)), ((), ()))
 
 
-CHUNKS = (("z", 0, 256), ("y", 256, 512), ("z", 768, 512), ("y", 1280, 256))
-N_SEMS = 320
+CHUNKS = (("y", 0, 256), ("z", 256, 256), ("y", 512, 512), ("z", 1024, 256), ("y", 1280, 256))
+N_SEMS = 360
+LAGS = ((2, (0, 1)),)
 LINK_RATE, LATENCY, ISSUE = 44e3, 2.3, 0.03
+
+ORDER = (
+    0, 1, 2, 58, 3, 46, 4, 57, 69, 7, 43, 35, 44, 47, 68, 8, 60, 13, 5, 10, 19, 45, 52, 53, 16, 49, 9, 6, 54, 11,
+    22, 48, 50, 42, 20, 36, 51, 28, 31, 25, 37, 12, 71, 59, 75, 14, 41, 72, 34, 79, 17, 56, 61, 90, 29, 38, 32, 26,
+    70, 40, 55, 80, 23, 64, 18, 21, 39, 15, 112, 33, 30, 65, 67, 27, 24, 113, 114, 115, 116, 63, 117, 81, 74, 78,
+    66, 62, 91, 118, 73, 76, 77, 101, 119, 83, 92, 120, 121, 122, 123, 124, 89, 82, 86, 85, 84, 125, 87, 88, 126,
+    144, 94, 141, 150, 98, 147, 138, 127, 93, 96, 135, 156, 128, 99, 186, 168, 172, 195, 177, 190, 153, 97, 100,
+    95, 181, 145, 199, 142, 102, 103, 129, 151, 148, 130, 219, 216, 187, 210, 196, 225, 182, 131, 132, 200, 104,
+    262, 108, 267, 258, 169, 213, 271, 240, 244, 253, 249, 143, 173, 191, 105, 157, 110, 152, 178, 109, 111, 149,
+    222, 197, 107, 106, 163, 183, 146, 220, 268, 259, 272, 263, 250, 241, 245, 133, 254, 134, 174, 291, 201, 159,
+    269, 154, 164, 184, 198, 217, 260, 297, 288, 179, 264, 223, 294, 273, 188, 158, 192, 221, 292, 160, 231, 214,
+    235, 255, 289, 251, 170, 228, 285, 202, 265, 155, 261, 218, 295, 226, 279, 270, 246, 293, 180, 303, 307, 211,
+    274, 224, 236, 232, 139, 252, 298, 193, 286, 229, 189, 215, 207, 290, 282, 296, 242, 256, 300, 308, 175, 165,
+    304, 203, 275, 185, 233, 227, 204, 212, 237, 299, 171, 257, 161, 247, 287, 283, 276, 194, 136, 305, 230, 309,
+    301, 243, 266, 234, 208, 166, 238, 205, 140, 280, 284, 162, 306, 176, 277, 302, 310, 248, 206, 137, 167, 209,
+    239, 278, 281, 311,
+)
 
 
 class Task:
@@ -54,7 +72,7 @@
 
 
 def kernel(
-    tok_hbm, ln_gain, wq, wm, q_gain, k_gain, ow, bias_in, mo,
+    tok_hbm, ln_gain, wq, wm, q_gain, k_gain, ow, bias_in, mo, out_bias,
     out,
     tok, stats, stats_in, xg, WQ, WM, BV, BI, OW, MO, hq, hm, hxq, hxm, att, part, *rest,
 ):
@@ -189,9 +207,11 @@
         stats[...] = jnp.where(row < 4, turned[0:1], turned[64:65])
 
     def bias_columns():
-        b = bias_in[...].astype(F32)
-        for i in range(2):
-            BV[pl.ds(i * 128, 128), :] = jnp.broadcast_to(b[i : i + 1], (128, 128)).T.astype(BF16)
+        for i, count in enumerate((128, 64)):
+            b = bias_in[pl.ds(i * 128, count)].astype(F32).reshape(1, count)
+            if count < 128:
+                b = jnp.concatenate([b, b], axis=1)
+            BV[pl.ds(i * 128, 128), :] = jnp.broadcast_to(b, (128, 128)).T.astype(BF16)
         mine = pl.ds(pl.multiple_of(yl * UNITS, 32), UNITS)
         BI[x] = BV[mine, :]
 
@@ -309,6 +329,9 @@
             after = [("x", "i", 0, 1), ("x", "i", 0, -1), ("w", "i"), ("x", "q", 1, 1), ("x", "q", 1, -1)]
         else:
             after = [("w2q", c - 1)] + ([("x", "i", 1, 1), ("x", "i", 1, -1)] if c == 1 else [])
+            for lag, qs in LAGS:
+                if c >= lag:
+                    after += [("x", (w, c - lag), q, d) for w in "om" for q in qs for d in (1, -1)]
         task(("w2p", c), deps=after, prio=7, pushes=x_push(pair[0], 0) + x_push(pair[1], 0))
         task(
             ("w2q", c), deps=[("w2s", c), ("w2p", c)], prio=7, takes=[w_take(w) for w in pair],
@@ -587,7 +610,8 @@
     for c in range(n):
         reduction(c)
 
-    for step in in_order(tasks):
+    assert sorted(ORDER) == list(range(len(tasks)))
+    for step in [tasks[i] for i in ORDER]:
         for key, ref in step.takes:
             take(key, ref())
         if step.body is not None:
@@ -596,7 +620,8 @@
             push(key, *refs())
 
     own = pl.ds(pl.multiple_of((z * 2 + yh) * BLOCK, BLOCK), BLOCK)
-    out[...] = part[yl, own]
+    g = out_bias[...].astype(F32)
+    out[...] = part[yl, own] + jnp.concatenate([g[i : i + 1] for i in range(PIECE // 128)], axis=1)
     for copy in started:
         copy.wait_send()
     assert len(index) <= N_SEMS, len(index)
@@ -608,8 +633,7 @@
     wq = jnp.transpose(qkv_weight, (1, 2, 3, 0))
     wm = jnp.transpose(mlp_in).reshape(2, UNITS, PIECE)
     mo = mlp_out.reshape(2, UNITS, PIECE)
-    bias = jnp.pad(mlp_bias, (0, 64)).reshape(2, 128)
-    vm, hbm = pl.BlockSpec(memory_space=pltpu.VMEM), pl.BlockSpec(memory_space=pl.ANY)
+    vm, hbm = pl.BlockSpec(memory_space=pltpu.VMEM), pl.BlockSpec(memory_space=pltpu.HBM)
     scratch = [
         pltpu.VMEM((BLOCK, PIECE), BF16),
         pltpu.VMEM((8, 128), F32),
@@ -642,7 +666,7 @@
     sums = pl.pallas_call(
         kernel,
         out_shape=jax.ShapeDtypeStruct((BLOCK, PIECE), F32),
-        in_specs=[hbm, vm, hbm, hbm, vm, vm, hbm, vm, hbm],
+        in_specs=[hbm, vm, hbm, hbm, vm, vm, hbm, vm, hbm, vm],
         out_specs=vm,
         scratch_shapes=scratch,
         compiler_params=pltpu.CompilerParams(
@@ -651,9 +675,10 @@
         name="layer",
     )(
         tokens, ln_gain.reshape(PIECE // 128, 128), wq, wm, q_gain.reshape(1, HD),
-        k_gain.reshape(1, HD), out_weight, bias, mo,
+        k_gain.reshape(1, HD), out_weight, mlp_bias, mo,
+        out_bias.reshape(PIECE // 128, 128),
     )
-    return tokens.astype(F32) + sums + out_bias.astype(F32)
+    return tokens.astype(F32) + sums
 
 
 def solution(mesh):

time: 123 us -> 115 us (0.935)
  Pallas kernels: 119 us -> 113 us
    pallas_call x1, Pallas kernels: 119 us -> 113 us  [per_device(): pl.pallas_call(kernel, out_shape=jax.ShapeDtypeStruct((BLOCK, PIECE), F32...]
where the time goes in v4:
time: 115 us
  Pallas kernels  113 us (98%)
  other arithmetic  1.78 us (2%)
    pallas_call x1, Pallas kernels, per_device(): pl.pallas_call(kernel, out_shape=jax.ShapeDtypeStruct((BLOCK, PIECE), F32...  113 us

profile of v4, /device:TPU:2, one launch (start us, length us, event | category | flops | bytes accessed | tf_op | source)
XLA Modules:
  0.0 115.1 jit_solution(14628038586143596857)
XLA Ops:
  0.0 0.0 copy-start
  0.0 113.3 %layer.1 = f32[64,1536]{1,0:T(8,128)} custom-call(bf16[64,1536]{1,0:T(8,128)(2,1)} %tok_hbm.1, bf16[12,128]{1,0:T(8,128)(2,1)} %bitcast.12, bf16[3,2,32,1536]{3,2,1,0:T(8,128)(2,1)} %bitcast.9, bf16[2,96,1536]{2,1,0:T(8,128)(2,1)} %bitcast.10, bf16[1,128]{1,0:T(2,128)(2,1)} %bitcast.14, bf16[1,128]{1,0:T(2,128)(2,1)} %bitcast.15, bf16[2,32,1536]{2,1,0:T(8,128)(2,1)} %ow.1, ...), custom_call_target="tpu_custom_call" | custom-call | tf_op jit(solution)/shard_map/layer/pallas_call | solution.py:666
  113.3 0.0 copy-done
  113.3 1.8 %convert_add_fusion = f32[64,1536]{1,0:T(8,128)} fusion(f32[64,1536]{1,0:T(8,128)} %layer.1, bf16[64,1536]{1,0:T(8,128)(2,1)S(1)} %copy-done), kind=kLoop, calls=%fused_computation | loop fusion | flops 196608 | bytes 983040 | tf_op jit(solution)/shard_map/add | solution.py:681
Async XLA Ops:
  0.0 113.3 %copy-start = (bf16[64,1536]{1,0:T(8,128)(2,1)S(1)}, bf16[64,1536]{1,0:T(8,128)(2,1)}, u32[]{:S(2)}) copy-start(bf16[64,1536]{1,0:T(8,128)(2,1)} %tok_hbm.1) | copy-start | bytes 589828

commit v5 on v4

--- a/solution.py
+++ b/solution.py
@@ -21,26 +21,26 @@
 NT = (((1,), (1,)), ((), ()))
 
 
-CHUNKS = (("y", 0, 256), ("z", 256, 256), ("y", 512, 512), ("z", 1024, 256), ("y", 1280, 256))
+CHUNKS = (("y", 0, 256), ("z", 256, 256), ("y", 512, 384), ("z", 896, 384), ("y", 1280, 256))
 N_SEMS = 360
 LAGS = ((2, (0, 1)),)
 LINK_RATE, LATENCY, ISSUE = 44e3, 2.3, 0.03
 
 ORDER = (
-    0, 1, 2, 58, 3, 46, 4, 57, 69, 7, 43, 35, 44, 47, 68, 8, 60, 13, 5, 10, 19, 45, 52, 53, 16, 49, 9, 6, 54, 11,
-    22, 48, 50, 42, 20, 36, 51, 28, 31, 25, 37, 12, 71, 59, 75, 14, 41, 72, 34, 79, 17, 56, 61, 90, 29, 38, 32, 26,
-    70, 40, 55, 80, 23, 64, 18, 21, 39, 15, 112, 33, 30, 65, 67, 27, 24, 113, 114, 115, 116, 63, 117, 81, 74, 78,
-    66, 62, 91, 118, 73, 76, 77, 101, 119, 83, 92, 120, 121, 122, 123, 124, 89, 82, 86, 85, 84, 125, 87, 88, 126,
-    144, 94, 141, 150, 98, 147, 138, 127, 93, 96, 135, 156, 128, 99, 186, 168, 172, 195, 177, 190, 153, 97, 100,
-    95, 181, 145, 199, 142, 102, 103, 129, 151, 148, 130, 219, 216, 187, 210, 196, 225, 182, 131, 132, 200, 104,
-    262, 108, 267, 258, 169, 213, 271, 240, 244, 253, 249, 143, 173, 191, 105, 157, 110, 152, 178, 109, 111, 149,
-    222, 197, 107, 106, 163, 183, 146, 220, 268, 259, 272, 263, 250, 241, 245, 133, 254, 134, 174, 291, 201, 159,
-    269, 154, 164, 184, 198, 217, 260, 297, 288, 179, 264, 223, 294, 273, 188, 158, 192, 221, 292, 160, 231, 214,
-    235, 255, 289, 251, 170, 228, 285, 202, 265, 155, 261, 218, 295, 226, 279, 270, 246, 293, 180, 303, 307, 211,
-    274, 224, 236, 232, 139, 252, 298, 193, 286, 229, 189, 215, 207, 290, 282, 296, 242, 256, 300, 308, 175, 165,
-    304, 203, 275, 185, 233, 227, 204, 212, 237, 299, 171, 257, 161, 247, 287, 283, 276, 194, 136, 305, 230, 309,
-    301, 243, 266, 234, 208, 166, 238, 205, 140, 280, 284, 162, 306, 176, 277, 302, 310, 248, 206, 137, 167, 209,
-    239, 278, 281, 311,
+    0, 1, 69, 58, 2, 3, 57, 68, 4, 7, 46, 79, 44, 49, 48, 43, 35, 5, 10, 8, 47, 53, 54, 71, 72, 25, 13, 60, 61, 45,
+    22, 6, 9, 16, 19, 11, 26, 42, 28, 36, 31, 14, 23, 34, 90, 101, 51, 50, 52, 59, 70, 17, 20, 27, 12, 41, 29, 32,
+    37, 112, 24, 15, 40, 113, 21, 18, 38, 114, 39, 55, 56, 80, 81, 65, 64, 75, 76, 62, 63, 30, 33, 66, 67, 73, 74,
+    78, 77, 91, 92, 115, 116, 117, 83, 82, 118, 119, 120, 87, 86, 121, 122, 123, 124, 84, 85, 89, 88, 125, 126,
+    127, 128, 168, 199, 144, 147, 177, 190, 94, 93, 181, 195, 153, 172, 156, 135, 141, 150, 138, 186, 98, 95, 97,
+    96, 169, 200, 99, 100, 102, 103, 145, 178, 148, 191, 196, 182, 173, 187, 157, 154, 129, 170, 201, 130, 179,
+    192, 136, 151, 222, 216, 219, 139, 197, 183, 131, 188, 174, 132, 267, 271, 149, 104, 109, 108, 105, 213, 146,
+    142, 225, 253, 249, 163, 262, 244, 159, 107, 106, 258, 240, 158, 202, 155, 110, 111, 152, 137, 193, 198, 184,
+    189, 180, 175, 171, 220, 210, 272, 268, 250, 254, 164, 160, 133, 140, 259, 263, 134, 291, 217, 223, 297, 241,
+    288, 245, 285, 294, 203, 194, 143, 185, 221, 235, 231, 176, 269, 273, 292, 226, 214, 300, 228, 282, 251, 255,
+    289, 161, 218, 295, 211, 207, 264, 279, 224, 293, 298, 307, 303, 232, 236, 165, 260, 227, 286, 204, 270, 274,
+    215, 252, 256, 290, 301, 296, 304, 242, 308, 246, 212, 233, 237, 229, 265, 261, 208, 283, 275, 257, 276, 280,
+    299, 309, 166, 287, 305, 162, 302, 205, 247, 243, 230, 234, 238, 284, 209, 266, 277, 306, 310, 206, 167, 281,
+    248, 239, 278, 311,
 )
 
 

time: 115 us -> 113 us (0.983)
  Pallas kernels: 113 us -> 111 us
    pallas_call x1, Pallas kernels: 113 us -> 111 us  [per_device(): pl.pallas_call(kernel, out_shape=jax.ShapeDtypeStruct((BLOCK, PIECE), F32...]
where the time goes in v5:
time: 113 us
  Pallas kernels  111 us (98%)
  other arithmetic  1.78 us (2%)
    pallas_call x1, Pallas kernels, per_device(): pl.pallas_call(kernel, out_shape=jax.ShapeDtypeStruct((BLOCK, PIECE), F32...  111 us

profile of v5, /device:TPU:2, one launch (start us, length us, event | category | flops | bytes accessed | tf_op | source)
XLA Modules:
  0.0 113.1 jit_solution(11790867117229837089)
XLA Ops:
  0.0 0.0 copy-start
  0.0 111.3 %layer.1 = f32[64,1536]{1,0:T(8,128)} custom-call(bf16[64,1536]{1,0:T(8,128)(2,1)} %tok_hbm.1, bf16[12,128]{1,0:T(8,128)(2,1)} %bitcast.12, bf16[3,2,32,1536]{3,2,1,0:T(8,128)(2,1)} %bitcast.9, bf16[2,96,1536]{2,1,0:T(8,128)(2,1)} %bitcast.10, bf16[1,128]{1,0:T(2,128)(2,1)} %bitcast.14, bf16[1,128]{1,0:T(2,128)(2,1)} %bitcast.15, bf16[2,32,1536]{2,1,0:T(8,128)(2,1)} %ow.1, ...), custom_call_target="tpu_custom_call" | custom-call | tf_op jit(solution)/shard_map/layer/pallas_call | solution.py:666
  111.3 0.0 copy-done
  111.3 1.8 %convert_add_fusion = f32[64,1536]{1,0:T(8,128)} fusion(f32[64,1536]{1,0:T(8,128)} %layer.1, bf16[64,1536]{1,0:T(8,128)(2,1)S(1)} %copy-done), kind=kLoop, calls=%fused_computation | loop fusion | flops 196608 | bytes 983040 | tf_op jit(solution)/shard_map/add | solution.py:681
Async XLA Ops:
  0.0 111.3 %copy-start = (bf16[64,1536]{1,0:T(8,128)(2,1)S(1)}, bf16[64,1536]{1,0:T(8,128)(2,1)}, u32[]{:S(2)}) copy-start(bf16[64,1536]{1,0:T(8,128)(2,1)} %tok_hbm.1) | copy-start | bytes 589828

commit v6 on v5

--- a/solution.py
+++ b/solution.py
@@ -22,25 +22,25 @@
 
 
 CHUNKS = (("y", 0, 256), ("z", 256, 256), ("y", 512, 384), ("z", 896, 384), ("y", 1280, 256))
-N_SEMS = 360
+N_SEMS = 400
 LAGS = ((2, (0, 1)),)
 LINK_RATE, LATENCY, ISSUE = 44e3, 2.3, 0.03
 
 ORDER = (
-    0, 1, 69, 58, 2, 3, 57, 68, 4, 7, 46, 79, 44, 49, 48, 43, 35, 5, 10, 8, 47, 53, 54, 71, 72, 25, 13, 60, 61, 45,
-    22, 6, 9, 16, 19, 11, 26, 42, 28, 36, 31, 14, 23, 34, 90, 101, 51, 50, 52, 59, 70, 17, 20, 27, 12, 41, 29, 32,
-    37, 112, 24, 15, 40, 113, 21, 18, 38, 114, 39, 55, 56, 80, 81, 65, 64, 75, 76, 62, 63, 30, 33, 66, 67, 73, 74,
-    78, 77, 91, 92, 115, 116, 117, 83, 82, 118, 119, 120, 87, 86, 121, 122, 123, 124, 84, 85, 89, 88, 125, 126,
-    127, 128, 168, 199, 144, 147, 177, 190, 94, 93, 181, 195, 153, 172, 156, 135, 141, 150, 138, 186, 98, 95, 97,
-    96, 169, 200, 99, 100, 102, 103, 145, 178, 148, 191, 196, 182, 173, 187, 157, 154, 129, 170, 201, 130, 179,
-    192, 136, 151, 222, 216, 219, 139, 197, 183, 131, 188, 174, 132, 267, 271, 149, 104, 109, 108, 105, 213, 146,
-    142, 225, 253, 249, 163, 262, 244, 159, 107, 106, 258, 240, 158, 202, 155, 110, 111, 152, 137, 193, 198, 184,
-    189, 180, 175, 171, 220, 210, 272, 268, 250, 254, 164, 160, 133, 140, 259, 263, 134, 291, 217, 223, 297, 241,
-    288, 245, 285, 294, 203, 194, 143, 185, 221, 235, 231, 176, 269, 273, 292, 226, 214, 300, 228, 282, 251, 255,
-    289, 161, 218, 295, 211, 207, 264, 279, 224, 293, 298, 307, 303, 232, 236, 165, 260, 227, 286, 204, 270, 274,
-    215, 252, 256, 290, 301, 296, 304, 242, 308, 246, 212, 233, 237, 229, 265, 261, 208, 283, 275, 257, 276, 280,
-    299, 309, 166, 287, 305, 162, 302, 205, 247, 243, 230, 234, 238, 284, 209, 266, 277, 306, 310, 206, 167, 281,
-    248, 239, 278, 311,
+    0, 1, 4, 5, 2, 3, 7, 8, 13, 6, 55, 14, 110, 53, 56, 57, 58, 52, 15, 16, 9, 19, 10, 22, 44, 63, 62, 31, 34, 51,
+    54, 28, 25, 17, 11, 12, 18, 66, 77, 59, 60, 23, 20, 61, 78, 67, 32, 45, 37, 40, 35, 29, 26, 46, 50, 21, 24,
+    121, 49, 123, 41, 47, 43, 88, 99, 38, 33, 36, 65, 64, 68, 79, 89, 80, 81, 30, 27, 125, 84, 85, 70, 69, 48, 74,
+    73, 39, 42, 127, 122, 71, 72, 124, 126, 75, 76, 90, 128, 82, 83, 129, 86, 87, 100, 101, 92, 91, 130, 96, 95,
+    131, 132, 133, 134, 93, 94, 135, 97, 98, 136, 137, 138, 209, 196, 157, 160, 187, 200, 102, 191, 103, 151, 145,
+    178, 163, 154, 205, 182, 148, 107, 106, 104, 105, 210, 197, 188, 158, 166, 161, 201, 109, 108, 192, 111, 112,
+    179, 183, 206, 152, 155, 139, 211, 198, 140, 202, 189, 146, 149, 229, 164, 232, 159, 226, 169, 193, 173, 180,
+    141, 184, 167, 114, 113, 235, 207, 223, 142, 281, 277, 263, 118, 117, 259, 268, 272, 254, 162, 250, 156, 153,
+    115, 116, 199, 119, 120, 150, 190, 203, 147, 194, 165, 181, 230, 238, 185, 208, 212, 278, 282, 170, 264, 174,
+    260, 168, 143, 269, 273, 144, 255, 251, 304, 301, 227, 233, 307, 295, 289, 298, 204, 195, 186, 231, 245, 241,
+    213, 283, 279, 302, 224, 236, 310, 220, 292, 265, 305, 261, 228, 299, 239, 217, 270, 274, 234, 308, 303, 317,
+    313, 242, 246, 296, 225, 214, 284, 280, 237, 266, 290, 175, 262, 252, 311, 306, 318, 256, 221, 300, 314, 171,
+    247, 275, 243, 271, 240, 285, 293, 267, 286, 218, 309, 319, 312, 176, 297, 315, 253, 215, 257, 222, 172, 294,
+    244, 291, 248, 276, 287, 320, 316, 216, 219, 258, 177, 288, 249, 321,
 )
 
 
@@ -275,7 +275,7 @@
     task(
         ("stats",), deps=[("begin",)], body=statistics, work=1.0, prio=-99,
         pushes=[stats_push(0, partner, "k"), stats_push(1, flip_l, "l"), stats_push(2, flip_lk, "l")]
-        + [w_push("q", 0)] + x_push("i", 0),
+        + [w_push("q", 0)],
     )
     task(
         ("bias",), deps=[("stats",)], body=bias_columns, work=0.3, prio=-98,
@@ -284,10 +284,11 @@
     task(
         ("norm",), deps=[("bias",)], body=normalise, work=0.8, prio=-97,
         takes=[(("stats", i), lambda i=i: stats_in.at[i]) for i in range(3)],
-        pushes=z_first(0, 0) + z_first(1, 0) + y_push(1, 0) + y_push(0, 0)
-        + [w_push("q", 1), w_push("i", 0)],
+        pushes=z_first(0, 0) + z_first(1, 0) + y_push(1, 0) + y_push(0, 0),
     )
-    gather = []
+    task(("xp", "i"), deps=[("stats",)], prio=-98.5, pushes=x_push("i", 0))
+    task(("w", "q", 1), deps=[("norm",)], prio=-90, pushes=[w_push("q", 1)])
+    task(("w", "i", 0), deps=[("w", "q", 1)], prio=-89, pushes=[w_push("i", 0)])
     for h in range(2):
         for r in range(1 if h == 0 else 4):
             for d in (1, -1):
@@ -295,8 +296,13 @@
                     task(
                         ("z", h, r, d, dist), deps=[("norm",)], prio=0 if h == 0 else 5,
                         takes=[z_take(h, r, d, dist)],
-                        pushes=[z_push(h, r, d, dist + 1)] + (y_push(0, -d * dist) if h == 0 else []),
+                        pushes=[z_push(h, r, d, dist + 1)],
                     )
+                    if h == 0:
+                        task(
+                            ("yp", (-d * dist) % NZ), deps=[("z", h, r, d, dist)], prio=0,
+                            pushes=y_push(0, -d * dist),
+                        )
     task(("z4",), takes=[z_take(0, 0, 1, 4), z_take(0, 0, -1, 4)], pushes=y_push(0, 4))
     for dz in range(NZ):
         task(
@@ -309,10 +315,10 @@
     )
     task(("yn", 1, 0), deps=[("norm",)], prio=2, takes=[y_take("yn", 1, 0)], pushes=z_first(1, 2))
     task(("yr", 1, 0), deps=[("norm",)], prio=2, takes=[y_take("yr", 1, 0)], pushes=z_first(1, 3))
-    task(("w", "i", 1), deps=[("z", 0, 0, 1, 1)], prio=3, pushes=[w_push("i", 1)])
+    task(("w", "i", 1), deps=[("z", 0, 0, 1, 1), ("w", "i", 0)], prio=3, pushes=[w_push("i", 1)])
     for w in ("q", "i"):
         task(
-            ("w", w), deps=[("norm",)] + ([("w", "i", 1)] if w == "i" else []), prio=2,
+            ("w", w), deps=[("norm",), ("w", w, 1)], prio=2,
             takes=[w_take(w, 0), w_take(w, 1)], pushes=x_push(w, 1),
         )
         x_relay(w, 0, [("norm",)])
@@ -370,25 +376,48 @@
             hq[r] = acc_q[i * 128 : (i + 1) * 128]
             hm[r] = acc_m[i * 128 : (i + 1) * 128]
 
-    def project_last(i):
-        row = pl.ds(pl.multiple_of(lax.rem(i * 256 + nk * 512, ROWS), 256), 256)
-        acc = hm[row]
+    def project_last(dzs):
+        rows = rows_of(dzs)
+        acc = jnp.concatenate([hm[r] for r in rows], axis=0)
         for h in range(2):
-            acc += product(xg[h, nl, row], WM.at[nl], h)
-        hm[row] = acc
-
-    def hq_refs():
-        return hq.at[pl.ds(pl.multiple_of(nk * 512, 512), 512)], hxq, partner
-
-    def hm_refs(i):
-        theirs = hm.at[pl.ds(pl.multiple_of(nk * 512 + i * 256, 256), 256)]
-        return theirs, hxm.at[pl.ds(i * 256, 256)], partner
-
+            acc += product(jnp.concatenate([xg[h, nl, r] for r in rows], axis=0), WM.at[nl], h)
+        for i, r in enumerate(rows):
+            hm[r] = acc[i * 128 : (i + 1) * 128]
+
+    def to_partner(kind, dz):
+        src, dst = (hq, hxq) if kind == "hq" else (hm, hxm)
+        zz = zn[dz % NZ]
+        there = pl.ds(pl.multiple_of(lax.rem(zz, NZ // 2) * 128, 128), 128)
+        return zz // (NZ // 2), src.at[rows_of((dz,))[0]], dst.at[there]
+
+    def send_sums(kind, dzs):
+        for dz in dzs:
+            owner, src, dst = to_partner(kind, dz)
+            i = index.setdefault((kind, dz), len(index))
+            copy = pltpu.make_async_remote_copy(
+                src_ref=src, dst_ref=dst, send_sem=send.at[i], recv_sem=recv.at[i],
+                device_id=partner, device_id_type=MESH,
+            )
+            pl.when(owner == nk)(copy.start)
+            sums_sent.append((owner, copy))
+
+    def take_sums(kind):
+        for dzs in groups:
+            for dz in dzs:
+                owner, _, dst = to_partner(kind, dz)
+                i = index[(kind, dz)]
+                copy = pltpu.make_async_remote_copy(
+                    src_ref=dst, dst_ref=dst, send_sem=send.at[i], recv_sem=recv.at[i],
+                    device_id=partner, device_id_type=MESH,
+                )
+                pl.when(owner == k)(copy.wait_recv)
+
+    sums_sent = []
     k_scale = LINK_RATE / 600e3
     early = x_last("q") + [t for t in x_last("i") if t[0][2] == 0]
     late = [t for t in x_last("i") if t[0][2] == 1]
     early_relays = [("x", w, q, d) for w, q in (("q", 0), ("q", 1), ("i", 0)) for d in (1, -1)]
-    late_relays = first_relays
+    late_relays = [("x", "i", 1, d) for d in (1, -1)]
     for g, dzs in enumerate(groups):
         takes, deps = (list(early), list(early_relays)) if g == 0 else ([], [("p", g - 1)])
         for dz in dzs:
@@ -403,16 +432,14 @@
                 d = -1 if dz > 0 else 1
                 deps += [("z", 0, 0, d, abs(dz))] + [("z", 1, r, d, abs(dz)) for r in range(4)]
         task(
-            ("p", g), takes=takes, deps=deps, body=lambda dzs=dzs: project(dzs), prio=30,
-            work=0.9 if len(dzs) == 1 else 1.4,
-            pushes=[(("hq",), "k", 512 * 384 * 4 * k_scale, hq_refs)] if g == 4 else [],
-        )
-    for i in range(4):
+            ("p", g), takes=takes, deps=deps, body=lambda dzs=dzs: (project(dzs), send_sums("hq", dzs)),
+            prio=30, work=0.9 if len(dzs) == 1 else 1.4, pushes=[(("hq", g), "k", 100e3 * k_scale, None)],
+        )
         task(
-            ("pl", i), takes=late if i == 0 else [],
-            deps=late_relays + [("p", 4)] if i == 0 else [("pl", i - 1)],
-            body=lambda i=i: project_last(i), work=0.5, prio=10,
-            pushes=[(("hm", i), "k", 256 * 384 * 4 * k_scale, lambda i=i: hm_refs(i))] if i < 2 else [],
+            ("pl", g), takes=late if g == 0 else [],
+            deps=late_relays + [("p", 0)] if g == 0 else [("pl", g - 1), ("p", g)],
+            body=lambda dzs=dzs: (project_last(dzs), send_sums("hm", dzs)), prio=31,
+            work=0.5 if len(dzs) == 1 else 0.67, pushes=[(("hm", g), "k", 100e3 * k_scale, None)],
         )
 
     def head_norm(values, gain):
@@ -450,16 +477,18 @@
 
     for i in range(2):
         task(
-            ("attend", i), deps=[("pl", 3)] + [("attend", 0)] * i, prio=10, work=0.45,
-            takes=[(("hq",), lambda: hxq)] if i == 0 else [], body=lambda i=i: attend(i),
+            ("attend", i), deps=first_relays + [("pl", 4)] + [("attend", 0)] * i, prio=10, work=0.45,
+            takes=[(("hq", g), None) for g in range(5)] if i == 0 else [],
+            body=lambda i=i: (take_sums("hq") if i == 0 else None, attend(i)),
         )
     for i in range(2):
-        takes = [(("hm", i), lambda i=i: hxm.at[pl.ds(i * 256, 256)])]
+        takes = []
         if i == 0:
-            takes += [(("bias", d), lambda d=d: BI.at[xs[-d % NX]]) for d in (1, -1, 2)]
+            takes = [(("bias", d), lambda d=d: BI.at[xs[-d % NX]]) for d in (1, -1, 2)]
+            takes += [(("hm", g), None) for g in range(5)]
         task(
             ("image", i), takes=takes, deps=[("attend", 1)] + [("image", 0)] * i, prio=10, work=0.45,
-            body=lambda i=i: activate(i),
+            body=lambda i=i: (take_sums("hm") if i == 0 else None, activate(i)),
             pushes=[(("att", i), "k", 256 * 512 * 2 * k_scale, lambda i=i: att_refs(i))],
         )
 
@@ -613,17 +642,21 @@
     assert sorted(ORDER) == list(range(len(tasks)))
     for step in [tasks[i] for i in ORDER]:
         for key, ref in step.takes:
-            take(key, ref())
+            if ref is not None:
+                take(key, ref())
         if step.body is not None:
             step.body()
         for key, _, _, refs in step.pushes:
-            push(key, *refs())
+            if refs is not None:
+                push(key, *refs())
 
     own = pl.ds(pl.multiple_of((z * 2 + yh) * BLOCK, BLOCK), BLOCK)
     g = out_bias[...].astype(F32)
     out[...] = part[yl, own] + jnp.concatenate([g[i : i + 1] for i in range(PIECE // 128)], axis=1)
     for copy in started:
         copy.wait_send()
+    for owner, copy in sums_sent:
+        pl.when(owner == nk)(copy.wait_send)
     assert len(index) <= N_SEMS, len(index)
 
 

time: 113 us -> 114 us (level)
  no operation moved by 1% of the time
where the time goes in v6:
time: 114 us
  Pallas kernels  112 us (98%)
  other arithmetic  1.78 us (2%)
    pallas_call x1, Pallas kernels, per_device(): pl.pallas_call(kernel, out_shape=jax.ShapeDtypeStruct((BLOCK, PIECE), F32...  112 us

profile of v6, /device:TPU:2, one launch (start us, length us, event | category | flops | bytes accessed | tf_op | source)
XLA Modules:
  0.0 114.1 jit_solution(12700632953338597200)
XLA Ops:
  0.0 0.0 copy-start
  0.0 112.3 %layer.1 = f32[64,1536]{1,0:T(8,128)} custom-call(bf16[64,1536]{1,0:T(8,128)(2,1)} %tok_hbm.1, bf16[12,128]{1,0:T(8,128)(2,1)} %bitcast.12, bf16[3,2,32,1536]{3,2,1,0:T(8,128)(2,1)} %bitcast.9, bf16[2,96,1536]{2,1,0:T(8,128)(2,1)} %bitcast.10, bf16[1,128]{1,0:T(2,128)(2,1)} %bitcast.14, bf16[1,128]{1,0:T(2,128)(2,1)} %bitcast.15, bf16[2,32,1536]{2,1,0:T(8,128)(2,1)} %ow.1, ...), custom_call_target="tpu_custom_call" | custom-call | tf_op jit(solution)/shard_map/layer/pallas_call | solution.py:699
  112.3 0.0 copy-done
  112.3 1.8 %convert_add_fusion = f32[64,1536]{1,0:T(8,128)} fusion(f32[64,1536]{1,0:T(8,128)} %layer.1, bf16[64,1536]{1,0:T(8,128)(2,1)S(1)} %copy-done), kind=kLoop, calls=%fused_computation | loop fusion | flops 196608 | bytes 983040 | tf_op jit(solution)/shard_map/add | solution.py:714
Async XLA Ops:
  0.0 112.3 %copy-start = (bf16[64,1536]{1,0:T(8,128)(2,1)S(1)}, bf16[64,1536]{1,0:T(8,128)(2,1)}, u32[]{:S(2)}) copy-start(bf16[64,1536]{1,0:T(8,128)(2,1)} %tok_hbm.1) | copy-start | bytes 589828
